TPU v7x, 32 devices: a 4x4x1 block of a 4x4x8 slice. The times are simulated.
32 devices in a mesh: batch: 1 (over z), ctx: 4 (over y), seq: 8 (over x, core).
Axes of the slice: x: 4, y: 4, z: 1, core: 2. Of those that a mesh axis runs over, the one named last changes fastest.
The devices are a block of a 4x4x8 slice.
Arguments:
- hidden: bfloat16 [16, 5120], P('batch')
- lengths: int32 [16], P('batch')
- latent_cache: bfloat16 [16, 8192, 512], P('batch', ('ctx', 'seq'))
- rope_keys: bfloat16 [16, 8192, 64], P('batch', ('ctx', 'seq'))
- w_uq: bfloat16 [5120, 128, 128], P(None, 'seq')
- w_qr: bfloat16 [5120, 128, 64], P(None, 'seq')
- w_uk: bfloat16 [128, 128, 512], P('seq')
- w_uv: bfloat16 [128, 512, 128], P('seq')
- w_out: bfloat16 [128, 128, 5120], P('seq')
Outputs:
- output: bfloat16 [16, 5120], P('batch')
All inputs are finite; a program needn't handle non-finite values.
Results may differ from a plain program's by a relative error of at most 0.00569913.
Values are sent between devices in bfloat16 or wider.
A program may use at most 768 MiB of HBM per device.

v0:
```python
import jax
import jax.numpy as jnp
from jax import lax
from jax.sharding import PartitionSpec as P

NEG_FILL = -1.0e30


def solution(mesh):
    seq_size = mesh.shape['seq']
    row_spec = P('batch', None)
    cache_spec = P('batch', ('ctx', 'seq'), None)
    proj_spec = P(None, 'seq', None)
    head_spec = P('seq', None, None)

    def local_step(hidden, lengths, latent_cache, rope_keys, w_uq, w_qr, w_uk, w_uv, w_out):
        t_local = latent_cache.shape[1]
        score_scale = (w_uq.shape[2] + w_qr.shape[2]) ** -0.5
        q_nope = jnp.einsum('bd,dhk->bhk', hidden, w_uq, preferred_element_type=jnp.float32).astype(jnp.bfloat16)
        q_rope = jnp.einsum('bd,dhr->bhr', hidden, w_qr, preferred_element_type=jnp.float32).astype(jnp.bfloat16)
        q_lat = jnp.einsum('bhk,hkc->bhc', q_nope, w_uk, preferred_element_type=jnp.float32).astype(jnp.bfloat16)
        lat_all = lax.all_gather(q_lat, 'seq', axis=1, tiled=True)
        rope_all = lax.all_gather(q_rope, 'seq', axis=1, tiled=True)
        scores = jnp.einsum('bhc,btc->bht', lat_all, latent_cache, preferred_element_type=jnp.float32)
        scores = (scores + jnp.einsum('bhr,btr->bht', rope_all, rope_keys, preferred_element_type=jnp.float32)) * score_scale
        shard_index = lax.axis_index('ctx') * seq_size + lax.axis_index('seq')
        positions = shard_index * t_local + jnp.arange(t_local)
        valid = positions[None, None, :] < lengths[:, None, None]
        scores = jnp.where(valid, scores, NEG_FILL)
        local_max = jnp.max(scores, axis=2)
        weights = jnp.where(valid, jnp.exp(scores - local_max[:, :, None]), 0.0)
        local_sum = jnp.sum(weights, axis=2)
        local_acc = jnp.einsum('bht,btc->bhc', weights.astype(jnp.bfloat16), latent_cache, preferred_element_type=jnp.float32)
        global_max = lax.pmax(local_max, ('ctx', 'seq'))
        rescale = jnp.exp(local_max - global_max)
        acc_heads = lax.psum_scatter(local_acc * rescale[:, :, None], 'seq', scatter_dimension=1, tiled=True)
        sum_heads = lax.psum_scatter(local_sum * rescale, 'seq', scatter_dimension=1, tiled=True)
        acc_heads = lax.psum(acc_heads, 'ctx')
        sum_heads = lax.psum(sum_heads, 'ctx')
        lat_out = (acc_heads / sum_heads[:, :, None]).astype(jnp.bfloat16)
        head_vals = jnp.einsum('bhc,hcv->bhv', lat_out, w_uv, preferred_element_type=jnp.float32).astype(jnp.bfloat16)
        mixed_part = jnp.einsum('bhv,hvd->bd', head_vals, w_out, preferred_element_type=jnp.float32)
        mixed = lax.psum(mixed_part, 'seq')
        return (hidden.astype(jnp.float32) + mixed).astype(jnp.bfloat16)

    return jax.shard_map(local_step, mesh=mesh,
                         in_specs=(row_spec, P('batch'), cache_spec, cache_spec, proj_spec, proj_spec, head_spec, head_spec, head_spec),
                         out_specs=row_spec, check_vma=False)
```

profile of v0, /device:TPU:97, one launch (start us, length us, event | category | flops | bytes accessed | tf_op | source)
XLA Modules:
  0.0 283.9 jit_solution(16445958653860379108)
XLA Ops:
  6.5 0.0 copy-start
  6.6 0.0 all-gather.2.cloned.1.call-start
  6.6 10.1 %fusion = bf16[16,16,128]{2,0,1:T(8,128)(2,1)S(1)} fusion(bf16[5120,16,128]{2,1,0:T(8,128)(2,1)} %param.13, bf16[16,5120]{1,0:T(8,128)(2,1)} %param.9), kind=kOutput, calls=%fused_computation | convolution fusion | flops 335544320 | bytes 21200896 | tf_op jit(solution)/shard_map/bd,dhk->bhk/dot_general | solution.py:19
  16.6 0.0 copy-start.2
  16.6 0.0 copy-done
  16.7 0.4 fusion.15
  17.0 0.9 copy.32
  17.9 0.1 all-gather.2.cloned.1.call-update
  18.0 0.1 reduce-scatter.5.cloned.1.call-start
  18.1 0.0 copy-done.2
  18.1 0.0 copy-start.4
  18.1 6.8 %fusion.12 = bf16[16,16,64]{2,0,1:T(8,128)(2,1)S(1)} fusion(bf16[5120,16,64]{0,2,1:T(8,128)(2,1)} %param.14, bf16[16,5120]{1,0:T(8,128)(2,1)S(1)} %copy-done.2), kind=kOutput, calls=%fused_computation.18 | convolution fusion | flops 167772160 | bytes 10682368 | tf_op jit(solution)/shard_map/bd,dhr->bhr/dot_general | solution.py:20
  24.9 22.4 %all_gather.7 = bf16[16,128,64]{2,1,0:T(8,128)(2,1)S(1)} all-gather(bf16[16,16,64]{2,1,0:T(8,128)(2,1)S(1)} %copy.30), channel_id=1, replica_groups=mesh['batch'=1,'ctx'=4,'seq'=8] {'seq'}, dimensions={1}, use_global_device_ids=true | all-gather | bytes 294912 | tf_op jit(solution)/shard_map/all_gather | solution.py:23
  47.3 0.0 copy-done.4
  47.3 0.1 broadcast_compare_fusion
  47.3 0.0 copy-start.3
  47.3 0.0 all-gather.2.cloned.1.call-done
  47.4 4.4 %fusion.20 = f32[16,128,256]{2,1,0:T(8,128)S(1)} fusion(bf16[16,128,512]{2,1,0:T(8,128)(2,1)} %all-gather.2.cloned.1.call-done, bf16[16,256,512]{2,1,0:T(8,128)(2,1)} %param.11), kind=kOutput, calls=%fused_computation.31 | convolution fusion | flops 536870912 | bytes 8388608 | tf_op jit(solution)/shard_map/bhc,btc->bht/dot_general | solution.py:24
  51.7 0.0 copy-done.3
  51.7 0.6 fusion.19
  52.3 50.2 %pmax.7 = f32[16,128]{1,0:T(8,128)S(1)} all-reduce(f32[16,128]{1,0:T(8,128)S(1)} %get-tuple-element.7), channel_id=1, replica_groups=mesh['batch'=1,'ctx'=4,'seq'=8] {'ctx','seq'}, use_global_device_ids=true, to_apply=%region_1.2 | all-reduce | flops 2048 | bytes 16384 | tf_op jit(solution)/shard_map/pmax | solution.py:34
  102.5 0.7 fusion.2
  103.2 5.5 %convolution_multiply_fusion = f32[16,128,512]{2,1,0:T(8,128)} fusion(bf16[16,256,512]{2,1,0:T(8,128)(2,1)} %param.11, f32[16,128]{1,0:T(8,128)S(1)} %get-tuple-element.6, f32[16,128,256]{2,1,0:T(8,128)S(1)} %get-tuple-element.8, f32[16,128]{1,0:T(8,128)S(1)} %get-tuple-element.7, pred[16,256]{1,0:T(8,128)(4,1)S(1)} %broadcast_compare_fusion), kind=kOutput, calls=%fused_computation.3 | convolution fusion | flops 539492352 | bytes 10506240 | tf_op jit(solution)/shard_map/bht,btc->bhc/dot_general | solution.py:33
  108.7 0.1 reduce-scatter.5.cloned.1.call-update
  108.7 0.1 reduce-scatter.7.cloned.1.call-start
  108.8 0.7 copy.16
  109.5 0.1 reduce-scatter.7.cloned.1.call-update
  109.6 0.1 all-reduce.3.cloned.1.call-start
  109.7 29.7 %reduce-scatter.5.cloned.1.call-done = f32[16,16,512]{2,1,0:T(8,128)} async-done(((f32[16,128,512]{2,1,0:T(8,128)}), f32[16,16,512]{2,1,0:T(8,128)}) %reduce-scatter.5.cloned.1.call-update) | async-done | bytes 524304 | tf_op jit(solution)/shard_map/reduce_scatter | solution.py:36
  139.3 0.1 all-reduce.3.cloned.1.call-update
  139.4 0.1 all-reduce.5.cloned.1.call-start
  139.5 29.3 %reduce-scatter.7.cloned.1.call-done = f32[16,16]{1,0:T(8,128)} async-done(((f32[128,16]{1,0:T(8,128)}), f32[16,16]{1,0:T(8,128)}) %reduce-scatter.7.cloned.1.call-update) | async-done | bytes 1040
  168.8 0.8 copy.17
  169.5 8.9 %psum.22 = f32[16,16]{1,0:T(8,128)S(1)} all-reduce(f32[16,16]{1,0:T(8,128)S(1)} %copy.17), channel_id=1, replica_groups=mesh['batch'=1,'ctx'=4,'seq'=8] {'ctx'}, use_global_device_ids=true, to_apply=%region_6.7 | all-reduce | flops 256 | bytes 2048 | tf_op jit(solution)/shard_map/psum | solution.py:39
  178.4 29.8 %all-reduce.3.cloned.1.call-done = f32[16,16,512]{2,1,0:T(8,128)} async-done(((f32[16,16,512]{2,1,0:T(8,128)}), f32[16,16,512]{2,1,0:T(8,128)}) %all-reduce.3.cloned.1.call-update) | async-done | bytes 524304 | tf_op jit(solution)/shard_map/psum | solution.py:38
  208.2 1.1 divide_convert_fusion
  209.4 0.0 copy-start.1
  209.4 10.3 %convolution_bitcast_fusion = f32[16,5120]{1,0:T(8,128)} fusion(bf16[16,128,5120]{2,1,0:T(8,128)(2,1)} %param.17, bf16[16,512,128]{2,1,0:T(8,128)(2,1)} %param.16, bf16[16,16,512]{2,1,0:T(8,128)(2,1)S(1)} %divide_convert_fusion), kind=kOutput, calls=%fused_computation.2 | convolution fusion | flops 369131520 | bytes 23658496 | tf_op jit(solution)/shard_map/bhv,hvd->bd/dot_general | solution.py:42
  219.7 0.1 all-reduce.5.cloned.1.call-update
  219.8 55.9 %all-reduce.5.cloned.1.call-done = f32[16,5120]{1,0:T(8,128)} async-done(((f32[16,5120]{1,0:T(8,128)}), f32[16,5120]{1,0:T(8,128)}) %all-reduce.5.cloned.1.call-update) | async-done | bytes 327696 | tf_op jit(solution)/shard_map/psum | solution.py:43
  275.6 1.7 add_convert_fusion
  277.3 0.0 copy-done.1
  (4 shorter events, 0.1 us)
Async XLA Ops:
  6.5 10.1 %copy-start = (bf16[16,128,512]{2,1,0:T(8,128)(2,1)S(1)}, bf16[16,128,512]{2,1,0:T(8,128)(2,1)}, u32[]{:S(2)}) copy-start(bf16[16,128,512]{2,1,0:T(8,128)(2,1)} %param.15) | copy-start | bytes 6291460
  6.6 40.8 %all-gather.2.cloned.1.call-start = ((), (), s32[]{:S(2)}) async-start(), calls=%async_computation.2 | async-start | bytes 2359296 | tf_op jit(solution)/shard_map/all_gather | solution.py:22
  16.6 1.4 copy-start.2
  18.0 121.4 %reduce-scatter.5.cloned.1.call-start = ((), (), s32[]{:S(2)}) async-start(), calls=%async_computation.3 | async-start | bytes 4718592 | tf_op jit(solution)/shard_map/reduce_scatter | solution.py:36
  18.1 29.2 %copy-start.4 = (s32[16]{0:T(128)S(1)}, s32[16]{0:T(128)}, u32[]{:S(2)}) copy-start(s32[16]{0:T(128)} %param.10) | copy-start | bytes 196
  47.3 4.4 %copy-start.3 = (bf16[16,256,64]{1,2,0:T(8,128)(2,1)S(1)}, bf16[16,256,64]{1,2,0:T(8,128)(2,1)}, u32[]{:S(2)}) copy-start(bf16[16,256,64]{1,2,0:T(8,128)(2,1)} %param.12) | copy-start | bytes 1572868
  108.7 60.0 %reduce-scatter.7.cloned.1.call-start = ((), (), s32[]{:S(2)}) async-start(), calls=%async_computation.6 | async-start | bytes 73728
  109.6 98.7 %all-reduce.3.cloned.1.call-start = ((), (), s32[]{:S(2)}) async-start(), calls=%async_computation.4 | async-start | bytes 1048576 | tf_op jit(solution)/shard_map/psum | solution.py:38
  139.4 136.2 %all-reduce.5.cloned.1.call-start = ((), (), s32[]{:S(2)}) async-start(), calls=%async_computation.5 | async-start | bytes 655360 | tf_op jit(solution)/shard_map/psum | solution.py:43
  209.4 67.9 %copy-start.1 = (bf16[16,128,512]{2,1,0:T(8,128)(2,1)S(1)}, bf16[16,128,512]{2,1,0:T(8,128)(2,1)}, u32[]{:S(2)}) copy-start(bf16[16,128,512]{2,1,0:T(8,128)(2,1)} %param.15) | copy-start | bytes 6291460
Sparse Core Ops, SparseCore 0:
  18.1 27.2 all-gather.1
  108.8 30.4 reduce-scatter.4
  141.6 27.1 reduce-scatter.6
  171.0 37.2 all-reduce.2
  219.9 55.7 all-reduce.4
where the time goes:
time: 285 us; the launch traced here: 284 us
  waiting for transfers between devices  145 us (51%)
  blocking collectives  81.4 us (29%)
  matrix products  37.9 us (13%)
  between operations  13.3 us (5%)
  other arithmetic  3.6 us (1%)
    psum x1, waiting for transfers between devices, local_step(): mixed = lax.psum(mixed_part, 'seq')  55.9 us
    pmax x1, blocking collectives, local_step(): global_max = lax.pmax(local_max, ('ctx', 'seq'))  50.2 us
    psum x1, waiting for transfers between devices, local_step(): acc_heads = lax.psum(acc_heads, 'ctx')  29.8 us
    reduce_scatter x1, waiting for transfers between devices, local_step(): lax.psum_scatter(local_acc * rescale[:, :, None], 'seq', scatter_dimensio...  29.7 us
    unnamed x6, waiting for transfers between devices  29.6 us
    all_gather x1, blocking collectives, local_step(): rope_all = lax.all_gather(q_rope, 'seq', axis=1, tiled=True)  22.4 us
    dot_general x1, matrix products, local_step(): jnp.einsum('bhv,hvd->bd', head_vals, w_out, preferred_element_type=jnp.fl...  10.3 us
    dot_general x1, matrix products, local_step(): jnp.einsum('bd,dhk->bhk', hidden, w_uq, preferred_element_type=jnp.float32)  10.1 us
  transfers between devices with their start and end apart: 5, of which 4 were waited for; matrix products, arithmetic and copies ran while one was open for 3% of the time, Pallas kernels for 0%

commit v1 on v0

v1 whole, which is shorter than its diff:
```python
import jax
import jax.numpy as jnp
from jax import lax
from jax.experimental import pallas as pl
from jax.experimental.pallas import tpu as pltpu
from jax.sharding import PartitionSpec as P

NEG_FILL = -1.0e30
LANES = 128
MESH = pl.DeviceIdType.MESH


def decode_kernel(ny, ns, lens, hidden, qn, qr, wuk, cache, rope, wuv, wout, out,
                  cacheb, ropeb, qbuf, part, inbox, wukb, wuvb, woutb, qscr, ybuf, yin, obuf,
                  lsem, csend, crecv, gsend, grecv, rsend, rrecv, ysend, yrecv, osend, orecv):
    nx = ns // 2
    y, s = lax.axis_index("ctx"), lax.axis_index("seq")
    x, c = s // 2, s % 2
    rb, hb = y // 2, y % 2
    t_own, latent = cache.shape[1], cache.shape[2]
    rope_dim = rope.shape[1]
    nope = LANES
    scale = (nope + rope_dim) ** -0.5
    n_pos = 2 * t_own
    cols = hidden.shape[1] // ns

    def at_y(d):
        return {"ctx": (y + d + ny) % ny, "seq": s}

    def at_x(d):
        return {"ctx": y, "seq": ((x + d + nx) % nx) * 2 + c}

    span = pl.ds(c * t_own, t_own)
    local = [
        pltpu.make_async_copy(wuk, wukb, lsem.at[0]),
        pltpu.make_async_copy(cache, cacheb.at[:, span], lsem.at[1]),
        pltpu.make_async_copy(rope, ropeb.at[:, :, span], lsem.at[2]),
        pltpu.make_async_copy(wuv, wuvb, lsem.at[3]),
        pltpu.make_async_copy(wout, woutb, lsem.at[4]),
    ]
    for copy in local[:3]:
        copy.start()

    barrier = pltpu.get_barrier_semaphore()
    for dy in range(ny):
        for ds in range(ns):
            if dy or ds:
                pl.semaphore_signal(barrier, inc=1, device_id={"ctx": (y + dy) % ny, "seq": (s + ds) % ns},
                                    device_id_type=MESH)
    pl.semaphore_wait(barrier, ny * ns - 1)

    mate = {"ctx": y, "seq": s + 1 - 2 * c}
    other = pl.ds((1 - c) * t_own, t_own)
    swap = [
        pltpu.make_async_remote_copy(cache, cacheb.at[:, span], csend.at[0], crecv.at[0], device_id=mate, device_id_type=MESH),
        pltpu.make_async_remote_copy(rope, ropeb.at[:, :, span], csend.at[1], crecv.at[1], device_id=mate, device_id_type=MESH),
    ]
    for copy in swap:
        copy.start()

    nh = qn.shape[1]
    half_h, half_b = nh // 2, qn.shape[0] // 2
    local[0].wait()
    qrows = qn[pl.ds(rb * half_b, half_b)].reshape(half_b * nh, nope)
    head_of = lax.broadcasted_iota(jnp.int32, (half_b * nh, nope), 0) % nh
    big = jnp.concatenate([jnp.where(head_of == h, qrows, jnp.zeros_like(qrows)) for h in range(nh)], axis=1)
    q_lat = jnp.dot(big, wukb[...], preferred_element_type=jnp.float32)
    qscr[:, 0:latent] = q_lat
    qscr[:, latent:latent + rope_dim] = qr[pl.ds(rb * half_b, half_b)].reshape(half_b * nh, rope_dim).astype(jnp.float32)
    qscr[:, latent + rope_dim:] = jnp.zeros((half_b * nh, qscr.shape[1] - latent - rope_dim), jnp.float32)
    for j in range(half_b // 2):
        rows = [qscr[pl.ds(pl.multiple_of((2 * j + i) * nh + hb * half_h, 8), half_h), :] for i in range(2)]
        qbuf[rb, j, hb, x] = jnp.concatenate(rows, axis=0).astype(jnp.bfloat16)

    sends = []

    def send(src, dst, ssem, rsem, to):
        copy = pltpu.make_async_remote_copy(src, dst, ssem, rsem, device_id=to, device_id_type=MESH)
        copy.start()
        sends.append(copy)

    def recv(dst, rsem):
        pltpu.make_async_remote_copy(dst, dst, rsem, rsem, device_id=mate, device_id_type=MESH).wait_recv()

    def rbhb(d):
        yy = (y + d + ny) % ny
        return yy // 2, yy % 2

    def xx(d):
        return (x + d + nx) % nx

    def unit_a(d, a):
        return qbuf.at[rb, a, hb, xx(d)]

    def unit_b(d, a):
        r_, h_ = rbhb(d)
        return qbuf.at[r_, 2 + a, h_, x]

    def line_a(d, a):
        r_, h_ = rbhb(d)
        return qbuf.at[r_, a, h_]

    def line_b(d, a):
        return qbuf.at[:, 2 + a, :, xx(d)]

    def gather_start(k, get, to):
        for a in range(2):
            for i, d in ((0, 1), (2, -1)):
                send(get(0, a), get(0, a), gsend.at[k, i + a], grecv.at[k, i + a], to(d))

    def gather_forward(k, get, to):
        recv(get(-1, 0), grecv.at[k, 0])
        send(get(-1, 0), get(-1, 0), gsend.at[k, 4], grecv.at[k, 4], to(1))
        recv(get(1, 1), grecv.at[k, 3])
        send(get(1, 1), get(1, 1), gsend.at[k, 5], grecv.at[k, 5], to(-1))

    def gather_finish(k, get, a):
        if a == 0:
            recv(get(1, 0), grecv.at[k, 2])
            recv(get(-2, 0), grecv.at[k, 4])
        else:
            recv(get(-1, 1), grecv.at[k, 1])
            recv(get(2, 1), grecv.at[k, 5])

    gather_start(0, unit_a, at_x)
    gather_start(1, unit_b, at_y)
    gather_forward(0, unit_a, at_x)
    gather_forward(1, unit_b, at_y)
    for a in range(2):
        gather_finish(0, unit_a, a)
        for i, d in ((0, 1), (2, -1)):
            send(line_a(0, a), line_a(0, a), gsend.at[2, i + a], grecv.at[2, i + a], at_y(d))
        gather_finish(1, unit_b, a)
        for i, d in ((0, 1), (2, -1)):
            send(line_b(0, a), line_b(0, a), gsend.at[3, i + a], grecv.at[3, i + a], at_x(d))
    for copy in local[3:]:
        copy.start()
    for copy in local[1:3]:
        copy.wait()
    recv(cacheb.at[:, other], crecv.at[0])
    recv(ropeb.at[:, :, other], crecv.at[1])
    gather_forward(2, line_a, at_y)
    gather_forward(3, line_b, at_x)
    gather_finish(2, line_a, 0)
    gather_finish(3, line_b, 0)

    base = (y * ns + 2 * x) * t_own
    n_head = qbuf.shape[2] * qbuf.shape[3] * 8
    lane = lax.broadcasted_iota(jnp.int32, (8, LANES), 1)
    n_slab = latent // LANES

    def stats(groups):
        tile = jnp.zeros((8, LANES), jnp.float32)
        for i, (m_, l_) in enumerate(groups):
            tile = jnp.where((lane >= 32 * i) & (lane < 32 * i + 16), m_, tile)
            tile = jnp.where((lane >= 32 * i + 16) & (lane < 32 * i + 32), l_, tile)
        return tile

    def attend(cls, r):
        j = cls + 2 * (r % 2)
        r_ = r // 2
        q2 = qbuf[r_, j].reshape(2 * n_head, qbuf.shape[5])
        res = []
        for i in range(2):
            b = 4 * r + 2 * cls + i
            sc = lax.dot_general(q2[:, 0:latent], cacheb[b], (((1,), (1,)), ((), ())), preferred_element_type=jnp.float32)
            sc = sc + jnp.dot(q2[:, latent:latent + rope_dim], ropeb[b], preferred_element_type=jnp.float32)
            groups = []
            for x_ in range(nx):
                for h_ in range(2):
                    k = (h_ * nx + x_) * 16 + 8 * i
                    groups.append(sc[k:k + 8])
            sc = jnp.concatenate(groups, axis=0) * scale
            pos = base + lax.broadcasted_iota(jnp.int32, (n_head, n_pos), 1)
            valid = pos < lens[b]
            sc = jnp.where(valid, sc, NEG_FILL)
            m = jnp.max(sc, axis=1, keepdims=True)
            w = jnp.where(valid, jnp.exp(sc - m), 0.0)
            l = jnp.sum(w, axis=1, keepdims=True)
            acc = jnp.dot(w.astype(jnp.bfloat16), cacheb[b], preferred_element_type=jnp.float32)
            res.append((m, l, acc))
        for x_ in range(nx):
            ml = []
            for g in range(4):
                m, l, acc = res[g // 2]
                k = 16 * x_ + 8 * (g % 2)
                ml.append((m[k:k + 8], l[k:k + 8]))
                for n in range(n_slab):
                    part[cls, r, x_, 32 * n + 8 * g:32 * n + 8 * g + 8, :] = acc[k:k + 8, LANES * n:LANES * n + LANES]
            part[cls, r, x_, 32 * n_slab:32 * n_slab + 8, :] = stats(ml)

    def merge(own, box):
        st, si = own[32 * n_slab:32 * n_slab + 8, :], box[32 * n_slab:32 * n_slab + 8, :]
        ml = []
        for g in range(4):
            m1, m2 = st[:, 32 * g:32 * g + 1], si[:, 32 * g:32 * g + 1]
            l1, l2 = st[:, 32 * g + 16:32 * g + 17], si[:, 32 * g + 16:32 * g + 17]
            m = jnp.maximum(m1, m2)
            e1, e2 = jnp.exp(m1 - m), jnp.exp(m2 - m)
            ml.append((m, l1 * e1 + l2 * e2))
            f1, f2 = jnp.broadcast_to(e1, (8, LANES)), jnp.broadcast_to(e2, (8, LANES))
            for n in range(n_slab):
                k = 32 * n + 8 * g
                own[k:k + 8, :] = own[k:k + 8, :] * f1 + box[k:k + 8, :] * f2
        own[32 * n_slab:32 * n_slab + 8, :] = stats(ml)

    def rs_send(cls, r, x_, i, to):
        send(part.at[cls, r, x_], inbox.at[cls, i], rsend.at[cls, i], rrecv.at[cls, i], to)

    def rs_merge(cls, r, x_, i):
        recv(inbox.at[cls, i], rrecv.at[cls, i])
        merge(part.at[cls, r, x_], inbox.at[cls, i])

    def yy(d):
        return (y + d + ny) % ny

    def a_first(r):
        sg = 1 - 2 * (r % 2)
        rs_send(0, r, xx(2), r, at_x(sg))
        rs_send(0, r, xx(-sg), 4 + 2 * r + (1 if sg > 0 else 0), at_x(-sg))

    def a_second(r):
        sg = 1 - 2 * (r % 2)
        rs_merge(0, r, xx(sg), r)
        rs_send(0, r, xx(sg), 4 + 2 * r + (0 if sg > 0 else 1), at_x(sg))

    attend(0, 0)
    a_first(0)
    attend(0, 2)
    a_first(2)
    attend(0, 1)
    a_first(1)
    a_second(0)
    attend(0, 3)
    a_first(3)
    a_second(2)
    gather_finish(2, line_a, 1)
    gather_finish(3, line_b, 1)

    attend(1, yy(2))
    for x_ in range(nx):
        rs_send(1, yy(2), x_, x_, at_y(1 - 2 * (x_ % 2)))
    a_second(1)
    a_second(3)
    attend(1, yy(1))
    for x_ in range(nx):
        if x_ % 2 == 0:
            rs_merge(1, yy(1), x_, x_)
        rs_send(1, yy(1), x_, 4 + 2 * x_, at_y(1))
    attend(1, yy(-1))
    for x_ in range(nx):
        if x_ % 2 == 1:
            rs_merge(1, yy(-1), x_, x_)
        rs_send(1, yy(-1), x_, 4 + 2 * x_ + 1, at_y(-1))

    def a_final(r):
        for i in range(2):
            k = 4 + 2 * r + i
            recv(inbox.at[0, k], rrecv.at[0, k])
            merge(part.at[0, r, x], inbox.at[0, k])

    def b_final(x_):
        for i in range(2):
            k = 4 + 2 * x_ + i
            recv(inbox.at[1, k], rrecv.at[1, k])
            merge(part.at[1, y, x_], inbox.at[1, k])

    sy, sx = 1 - 2 * (x % 2), 1 - 2 * (y % 2)
    a_final(yy(2))
    rs_send(0, yy(2), x, 12, at_y(sy))
    attend(1, y)
    a_final(yy(-sy))
    rs_send(0, yy(-sy), x, 13, at_y(-sy))
    b_final(xx(2))
    rs_send(1, y, xx(2), 12, at_x(sx))
    a_final(yy(sy))
    rs_merge(0, yy(sy), x, 12)
    rs_send(0, yy(sy), x, 14, at_y(sy))
    b_final(xx(-sx))
    rs_send(1, y, xx(-sx), 13, at_x(-sx))
    b_final(xx(sx))
    rs_merge(1, y, xx(sx), 12)
    rs_send(1, y, xx(sx), 14, at_x(sx))
    a_final(y)
    b_final(x)
    for i in (13, 14):
        rs_merge(0, y, x, i)
        rs_merge(1, y, x, i)

    rows = []
    for cls in range(2):
        own = part.at[cls, y, x]
        st = own[32 * n_slab:32 * n_slab + 8, :]
        for g in range(4):
            inv = jnp.broadcast_to(st[:, 32 * g + 16:32 * g + 17], (8, LANES))
            rows.append(jnp.concatenate([own[32 * n + 8 * g:32 * n + 8 * g + 8, :] / inv for n in range(n_slab)], axis=1))
    o_l = jnp.concatenate(rows, axis=0).astype(jnp.bfloat16)
    n_own = o_l.shape[0]
    local[3].wait()
    head_o = lax.broadcasted_iota(jnp.int32, (n_own, wuv.shape[2]), 0) % nh
    v = jnp.zeros((n_own, wuv.shape[2]), jnp.float32)
    for h in range(nh):
        v = jnp.where(head_o == h, jnp.dot(o_l, wuvb[h], preferred_element_type=jnp.float32), v)
    v = v.astype(jnp.bfloat16)
    pi = lax.broadcasted_iota(jnp.int32, (16 * nh, n_own), 0)
    pj = lax.broadcasted_iota(jnp.int32, (16 * nh, n_own), 1)
    perm = jnp.where((pj % nh == pi // 16) & (pj // nh == pi % 16), 1.0, 0.0).astype(jnp.bfloat16)
    vp = jnp.dot(perm, v, preferred_element_type=jnp.float32).astype(jnp.bfloat16)
    lhs = jnp.concatenate([vp[16 * h:16 * h + 16] for h in range(nh)], axis=1)
    local[4].wait()
    n_rows = n_own // nh
    for k in range(1, ns + 1):
        s_ = (s + k) % ns
        piece = jnp.dot(lhs, woutb[:, pl.ds(pl.multiple_of(s_ * cols, LANES), cols)], preferred_element_type=jnp.float32)
        if k < ns:
            ybuf[k] = piece[0:n_rows]
            send(ybuf.at[k], yin.at[ns - k], ysend.at[k], yrecv.at[ns - k], {"ctx": y, "seq": s_})
        else:
            total = piece[0:n_rows]
    for k in range(1, ns):
        recv(yin.at[k], yrecv.at[k])
        total = total + yin[k]
    hid = hidden[:, pl.ds(pl.multiple_of(s * cols, LANES), cols)].astype(jnp.float32)
    mine = hid[0:n_rows]
    for y_ in range(1, ny):
        mine = jnp.where(y == y_, hid[n_rows * y_:n_rows * y_ + n_rows], mine)
    obuf[y * ns + s] = (mine + total).astype(jnp.bfloat16)
    me = y * ns + s
    for k in range(1, ny * ns):
        to = (me + k) % (ny * ns)
        send(obuf.at[me], obuf.at[me], osend.at[k], orecv.at[k], {"ctx": to // ns, "seq": to % ns})
    for k in range(1, ny * ns):
        recv(obuf.at[(me + ny * ns - k) % (ny * ns)], orecv.at[k])
    out[...] = obuf[...]
    for copy in sends:
        copy.wait_send()
    for copy in swap:
        copy.wait_send()


def solution(mesh):
    ny, ns = mesh.shape['ctx'], mesh.shape['seq']
    row_spec = P('batch', None)
    cache_spec = P('batch', ('ctx', 'seq'), None)
    proj_spec = P(None, 'seq', None)
    head_spec = P('seq', None, None)

    def local_step(hidden, lengths, latent_cache, rope_keys, w_uq, w_qr, w_uk, w_uv, w_out):
        q_nope = jnp.einsum('bd,dhk->bhk', hidden, w_uq, preferred_element_type=jnp.float32).astype(jnp.bfloat16)
        q_rope = jnp.einsum('bd,dhr->bhr', hidden, w_qr, preferred_element_type=jnp.float32).astype(jnp.bfloat16)
        rope_t = jnp.transpose(rope_keys, (0, 2, 1))
        nb, d_model = hidden.shape
        t_own, latent = latent_cache.shape[1:]
        nh = w_uq.shape[1]
        rope_dim = rope_t.shape[1]
        nx = ns // 2
        cols = d_model // ns
        n_rows = nb // ny
        bf, f32 = jnp.bfloat16, jnp.float32
        unit = (latent // LANES) * 32 + 8
        wide = latent + LANES
        dma = pltpu.SemaphoreType.DMA
        vmem = pl.BlockSpec(memory_space=pltpu.VMEM)
        anyw = pl.BlockSpec(memory_space=pl.ANY)
        import functools
        out = pl.pallas_call(
            functools.partial(decode_kernel, ny, ns),
            out_shape=jax.ShapeDtypeStruct((ny * ns, n_rows, cols), bf),
            in_specs=[pl.BlockSpec(memory_space=pltpu.SMEM), vmem, vmem, vmem, anyw, anyw, anyw, anyw, anyw],
            out_specs=vmem,
            scratch_shapes=[
                pltpu.VMEM((nb, 2 * t_own, latent), bf),
                pltpu.VMEM((nb, rope_dim, 2 * t_own), bf),
                pltpu.VMEM((2, nb // 4, 2, nx, 16, wide), bf),
                pltpu.VMEM((2, ny, nx, unit, LANES), f32),
                pltpu.VMEM((2, 15, unit, LANES), f32),
                pltpu.VMEM((w_uk.shape[0] * w_uk.shape[1], latent), bf),
                pltpu.VMEM(w_uv.shape, bf),
                pltpu.VMEM((w_out.shape[0] * w_out.shape[1], d_model), bf),
                pltpu.VMEM((nb // 2 * nh, wide), f32),
                pltpu.VMEM((ns, n_rows, cols), f32),
                pltpu.VMEM((ns, n_rows, cols), f32),
                pltpu.VMEM((ny * ns, n_rows, cols), bf),
                dma((5,)), dma((2,)), dma((2,)), dma((4, 6)), dma((4, 6)), dma((2, 15)), dma((2, 15)),
                dma((ns,)), dma((ns,)), dma((ny * ns,)), dma((ny * ns,)),
            ],
            compiler_params=pltpu.CompilerParams(collective_id=0, has_side_effects=True, vmem_limit_bytes=60 * 2 ** 20),
        )(lengths, hidden, q_nope, q_rope, w_uk.reshape(-1, latent), latent_cache, rope_t, w_uv, w_out.reshape(-1, d_model))
        out = out.reshape(ny, ns, n_rows, cols)
        return jnp.transpose(out, (0, 2, 1, 3)).reshape(nb, d_model)

    return jax.shard_map(local_step, mesh=mesh,
                         in_specs=(row_spec, P('batch'), cache_spec, cache_spec, proj_spec, proj_spec, head_spec, head_spec, head_spec),
                         out_specs=row_spec, check_vma=False)
```

time: 285 us -> 85.4 us (0.30)
  waiting for transfers between devices: 145 us -> 0 us
  blocking collectives: 81.4 us -> 0 us
  Pallas kernels: 0 us -> 67.9 us
  matrix products: 37.9 us -> 14.4 us
  between operations: 13.3 us -> 0.02 us
  other arithmetic: 3.6 us -> 0 us
    psum x2 -> x0, waiting for transfers between devices: 85.7 us -> none  [the longest x1 55.9 us: local_step(): mixed = lax.psum(mixed_part, 'seq')]
    pallas_call x0 -> x1, Pallas kernels: none -> 67.9 us  [local_step(): pl.pallas_call(functools.partial(decode_kernel, ny, ns), out_shape=jax.Sh...]
    pmax x1 -> x0, blocking collectives: 50.2 us -> none  [local_step(): global_max = lax.pmax(local_max, ('ctx', 'seq'))]
    reduce_scatter x1 -> x0, waiting for transfers between devices: 29.7 us -> none  [local_step(): lax.psum_scatter(local_acc * rescale[:, :, None], 'seq', scatter_dimensio...]
    unnamed x6 -> x0, waiting for transfers between devices: 29.6 us -> none
    all_gather x1 -> x0, blocking collectives: 22.4 us -> none  [local_step(): rope_all = lax.all_gather(q_rope, 'seq', axis=1, tiled=True)]
    dot_general x5 -> x0, matrix products: 21 us -> none  [the longest x1 10.3 us: local_step(): jnp.einsum('bhv,hvd->bd', head_vals, w_out, preferred_element_type=jnp.fl...]
    psum x1 -> x0, blocking collectives: 8.9 us -> none  [local_step(): sum_heads = lax.psum(sum_heads, 'ctx')]
  transfers between devices with their start and end apart: 5 -> 0, of which waited for: 4 -> 0; matrix products, arithmetic and copies ran while one was open for 3% -> 0% of each run, Pallas kernels for 0% -> 0%
where the time goes in v1:
time: 85.4 us; the launch traced here: 85.2 us
  Pallas kernels  67.9 us (80%)
  matrix products  14.4 us (17%)
  local copies, waits for them, and re-layouts  2.93 us (3%)
    pallas_call x1, Pallas kernels, local_step(): pl.pallas_call(functools.partial(decode_kernel, ny, ns), out_shape=jax.Sh...  67.9 us
    dot_general x1, matrix products, local_step(): jnp.einsum('bd,dhk->bhk', hidden, w_uq, preferred_element_type=jnp.float32)  10.2 us
    dot_general x1, matrix products, local_step(): jnp.einsum('bd,dhr->bhr', hidden, w_qr, preferred_element_type=jnp.float32)  4.15 us

profile of v1, /device:TPU:97, one launch (start us, length us, event | category | flops | bytes accessed | tf_op | source)
XLA Modules:
  0.0 85.2 jit_solution(13189082720685931761)
XLA Ops:
  0.0 0.0 copy-start
  0.0 0.0 copy-start.1
  0.0 10.2 %fusion = bf16[16,16,128]{2,0,1:T(8,128)(2,1)S(1)} fusion(bf16[5120,16,128]{2,1,0:T(8,128)(2,1)} %param.13, bf16[16,5120]{1,0:T(8,128)(2,1)} %hidden.1), kind=kOutput, calls=%fused_computation | convolution fusion | flops 335544320 | bytes 21200896 | tf_op jit(solution)/shard_map/bd,dhk->bhk/dot_general | solution.py:349
  10.2 0.7 copy.20.qn
  10.9 0.0 copy-done
  10.9 0.0 copy-done.1
  10.9 4.2 %fusion.2 = bf16[16,16,64]{2,0,1:T(8,128)(2,1)S(1)} fusion(bf16[5120,16,64]{0,2,1:T(8,128)(2,1)S(1)} %copy-done, bf16[16,5120]{1,0:T(8,128)(2,1)S(1)} %copy-done.1), kind=kOutput, calls=%fused_computation.2 | convolution fusion | flops 167772160 | bytes 10682368 | tf_op jit(solution)/shard_map/bd,dhr->bhr/dot_general | solution.py:350
  15.0 0.7 copy.19.qr
  15.7 67.9 %shard_map.91 = bf16[32,4,640]{2,1,0:T(4,128)(2,1)} custom-call(s32[16]{0:T(128)} %lens.1, bf16[16,5120]{1,0:T(8,128)(2,1)} %hidden.1, bf16[16,16,128]{2,1,0:T(8,128)(2,1)} %copy.20.qn, bf16[16,16,64]{2,1,0:T(8,128)(2,1)} %copy.19.qr, bf16[2048,512]{1,0:T(8,128)(2,1)} %bitcast.16, bf16[16,256,512]{2,1,0:T(8,128)(2,1)} %cache.1, ...), custom_call_target="tpu_custom_call" | custom-call | tf_op jit(solution)/shard_map/pallas_call | solution.py:366
  83.6 0.9 %copy.13 = bf16[4,4,8,640]{3,2,1,0:T(8,128)(2,1)S(1)} copy(bf16[4,4,8,640]{3,1,2,0:T(4,128)(2,1)} %bitcast.18) | data formatting | bytes 327680 | tf_op jit(solution)/shard_map/transpose | solution.py:390
  84.6 0.7 copy.14
Async XLA Ops:
  0.0 10.9 %copy-start = (bf16[5120,16,64]{0,2,1:T(8,128)(2,1)S(1)}, bf16[5120,16,64]{0,2,1:T(8,128)(2,1)}, u32[]{:S(2)}) copy-start(bf16[5120,16,64]{0,2,1:T(8,128)(2,1)} %param.14) | copy-start | bytes 31457284
  0.0 10.9 %copy-start.1 = (bf16[16,5120]{1,0:T(8,128)(2,1)S(1)}, bf16[16,5120]{1,0:T(8,128)(2,1)}, u32[]{:S(2)}) copy-start(bf16[16,5120]{1,0:T(8,128)(2,1)} %hidden.1) | copy-start | bytes 491524

commit v2 on v1

v2 whole, which is shorter than its diff:
```python
import jax
import jax.numpy as jnp
from jax import lax
from jax.experimental import pallas as pl
from jax.experimental.pallas import tpu as pltpu
from jax.sharding import PartitionSpec as P

NEG_FILL = -1.0e30
LANES = 128
MESH = pl.DeviceIdType.MESH


def decode_kernel(ny, ns, lens, hidden, wuq, wqr, wuk, cache, rope, wuv, wout, out,
                  cacheb, ropeb, qbuf, part, inbox, wukb, wuvb, woutb, wuqb, wqrb, hrep, ybuf, yin, obuf,
                  lsem, usem, qsem, csend, crecv, gsend, grecv, rsend, rrecv, ysend, yrecv, osend, orecv):
    nx = ns // 2
    y, s = lax.axis_index("ctx"), lax.axis_index("seq")
    x, c = s // 2, s % 2
    rb, hb = y // 2, y % 2
    t_own, latent = cache.shape[1], cache.shape[2]
    rope_dim = rope.shape[1]
    nope = wuq.shape[3]
    d_model = hidden.shape[1]
    nh = wuk.shape[0]
    half_h = wuq.shape[2]
    nb = hidden.shape[0]
    half_b = nb // 2
    scale = (nope + rope_dim) ** -0.5
    n_pos = 2 * t_own
    cols = hidden.shape[1] // ns

    def at_y(d):
        return {"ctx": (y + d + ny) % ny, "seq": s}

    def at_x(d):
        return {"ctx": y, "seq": ((x + d + nx) % nx) * 2 + c}

    step = 256
    n_step = d_model // step
    r_step = 2
    group = 4
    uq = [pltpu.make_async_copy(wuq.at[pl.ds(k * step * group, step * group), hb], wuqb.at[pl.ds(k * step * group, step * group)], usem.at[k])
          for k in range(n_step // group)]
    qr = [pltpu.make_async_copy(wqr.at[pl.ds(hb * half_h + k * r_step, r_step)], wqrb.at[pl.ds(k * r_step, r_step)], qsem.at[k])
          for k in range(half_h // r_step)]
    span = pl.ds(c * t_own, t_own)
    local = [
        pltpu.make_async_copy(wuk.at[pl.ds(hb * half_h, half_h)], wukb, lsem.at[0]),
        pltpu.make_async_copy(cache, cacheb.at[:, span], lsem.at[1]),
        pltpu.make_async_copy(rope, ropeb.at[:, :, span], lsem.at[2]),
        pltpu.make_async_copy(wuv, wuvb, lsem.at[3]),
        pltpu.make_async_copy(wout, woutb, lsem.at[4]),
    ]
    for copy in qr + uq:
        copy.start()

    barrier = pltpu.get_barrier_semaphore()
    for dy in range(ny):
        for ds in range(ns):
            if dy or ds:
                pl.semaphore_signal(barrier, inc=1, device_id={"ctx": (y + dy) % ny, "seq": (s + ds) % ns},
                                    device_id_type=MESH)

    wide_k = step * half_h
    si = lax.broadcasted_iota(jnp.int32, (2 * half_b, nb), 0)
    sj = lax.broadcasted_iota(jnp.int32, (2 * half_b, nb), 1)
    own_rows = jnp.where(sj == rb * half_b + si % half_b, 1.0, 0.0).astype(jnp.bfloat16)
    hid2 = jnp.dot(own_rows, hidden[...], preferred_element_type=jnp.float32).astype(jnp.bfloat16)
    stack = jnp.concatenate([hid2[:, step * k:step * k + step] for k in range(n_step)], axis=0)
    for n in range(half_h):
        ri = lax.broadcasted_iota(jnp.int32, (step, step), 0)
        rj = lax.broadcasted_iota(jnp.int32, (step, step), 1)
        spread = jnp.where(ri == (rj + n * step) // half_h, 1.0, 0.0).astype(jnp.bfloat16)
        hrep[:, n * step:(n + 1) * step] = jnp.dot(stack, spread, preferred_element_type=jnp.float32).astype(jnp.bfloat16)

    pl.semaphore_wait(barrier, ny * ns - 1)

    mate = {"ctx": y, "seq": s + 1 - 2 * c}
    other = pl.ds((1 - c) * t_own, t_own)
    swap = [
        pltpu.make_async_remote_copy(cache, cacheb.at[:, span], csend.at[0], crecv.at[0], device_id=mate, device_id_type=MESH),
        pltpu.make_async_remote_copy(rope, ropeb.at[:, :, span], csend.at[1], crecv.at[1], device_id=mate, device_id_type=MESH),
    ]
    for copy in swap:
        copy.start()

    q_rope = []
    for copy in qr:
        copy.wait()
    for k in range(half_h // r_step):
        w = wqrb[k * r_step:(k + 1) * r_step].reshape(r_step * rope_dim, d_model)
        q_rope.append(lax.dot_general(w, hid2, (((1,), (1,)), ((), ())), preferred_element_type=jnp.float32))
    q_rope = jnp.concatenate(q_rope, axis=0).T
    q_rope = jnp.concatenate([q_rope[0:half_b, rope_dim * h:rope_dim * (h + 1)] for h in range(half_h)], axis=0).astype(jnp.bfloat16)
    lane_h = lax.broadcasted_iota(jnp.int32, (2 * half_b, wide_k), 1) % half_h
    row_h = lax.broadcasted_iota(jnp.int32, (2 * half_b, wide_k), 0) // half_b
    sums = [jnp.zeros((half_h * half_b, nope), jnp.float32) for _ in range(2)]
    for g in range(n_step // group):
        uq[g].wait()
        for k in range(g * group, (g + 1) * group):
            hr = hrep[2 * half_b * k:2 * half_b * (k + 1), :]
            lhs = jnp.concatenate([jnp.where(lane_h == row_h + h, hr, jnp.zeros_like(hr)) for h in range(0, half_h, 2)], axis=0)
            w = wuqb[k * step:(k + 1) * step].reshape(wide_k, nope)
            sums[k % 2] = sums[k % 2] + jnp.dot(lhs, w, preferred_element_type=jnp.float32)
        if g == 2:
            for copy in local[:3]:
                copy.start()
    q_nope = (sums[0] + sums[1]).astype(jnp.bfloat16)

    n_q = half_b * half_h
    qi = lax.broadcasted_iota(jnp.int32, (n_q, n_q), 0)
    qj = lax.broadcasted_iota(jnp.int32, (n_q, n_q), 1)
    pick = jnp.where((qi % half_h == qj // half_b) & (qi // half_h == qj % half_b), 1.0, 0.0).astype(jnp.bfloat16)
    q_nope = jnp.dot(pick, q_nope, preferred_element_type=jnp.float32).astype(jnp.bfloat16)
    q_rope = jnp.dot(pick, q_rope, preferred_element_type=jnp.float32).astype(jnp.bfloat16)
    head_of = lax.broadcasted_iota(jnp.int32, (n_q, nope), 0) % half_h
    big = jnp.concatenate([jnp.where(head_of == h, q_nope, jnp.zeros_like(q_nope)) for h in range(half_h)], axis=1)
    local[0].wait()
    q_lat = jnp.dot(big, wukb[...].reshape(half_h * nope, latent), preferred_element_type=jnp.float32).astype(jnp.bfloat16)
    q_rope = jnp.concatenate([q_rope, jnp.zeros((n_q, LANES - rope_dim), jnp.bfloat16)], axis=1)
    for j in range(half_b // 2):
        qbuf[rb, j, hb, x, :, 0:latent] = q_lat[16 * j:16 * j + 16]
        qbuf[rb, j, hb, x, :, latent:] = q_rope[16 * j:16 * j + 16]

    sends = []

    def send(src, dst, ssem, rsem, to):
        copy = pltpu.make_async_remote_copy(src, dst, ssem, rsem, device_id=to, device_id_type=MESH)
        copy.start()
        sends.append(copy)

    def recv(dst, rsem):
        pltpu.make_async_remote_copy(dst, dst, rsem, rsem, device_id=mate, device_id_type=MESH).wait_recv()

    def rbhb(d):
        yy = (y + d + ny) % ny
        return yy // 2, yy % 2

    def xx(d):
        return (x + d + nx) % nx

    def cell(j, d1, d2):
        d_y, d_x = (d2, d1) if j < 2 else (d1, d2)
        r_, h_ = rbhb(-d_y)
        return qbuf.at[r_, j, h_, xx(-d_x)]

    def hop(j, stage, ref, along_x):
        for d in (2, 1, 3):
            send(ref, ref, gsend.at[j, stage, d], grecv.at[j, stage, d], at_x(d) if along_x else at_y(d))

    for a in range(2):
        for j in (a, a + 2):
            hop(j, 0, cell(j, 0, 0), j < 2)
        for j in (a, a + 2):
            hop(j, 1, cell(j, 0, 0), j >= 2)
    for a in range(2):
        for e in (1, 3, 2):
            for j in (a, a + 2):
                recv(cell(j, e, 0), grecv.at[j, 0, e])
                hop(j, 1 + e, cell(j, e, 0), j >= 2)

    def gather_finish(j):
        for e in range(4):
            for d in (1, 3, 2):
                recv(cell(j, e, d), grecv.at[j, 1 + e, d])

    for copy in local[3:]:
        copy.start()
    for copy in local[1:3]:
        copy.wait()
    recv(cacheb.at[:, other], crecv.at[0])
    recv(ropeb.at[:, :, other], crecv.at[1])
    gather_finish(0)
    gather_finish(2)

    base = (y * ns + 2 * x) * t_own
    n_head = qbuf.shape[2] * qbuf.shape[3] * 8
    lane = lax.broadcasted_iota(jnp.int32, (8, LANES), 1)
    n_slab = latent // LANES

    def stats(groups):
        tile = jnp.zeros((8, LANES), jnp.float32)
        for i, (m_, l_) in enumerate(groups):
            tile = jnp.where((lane >= 32 * i) & (lane < 32 * i + 16), m_, tile)
            tile = jnp.where((lane >= 32 * i + 16) & (lane < 32 * i + 32), l_, tile)
        return tile

    def attend(cls, r):
        j = cls + 2 * (r % 2)
        r_ = r // 2
        q2 = qbuf[r_, j].reshape(2 * n_head, qbuf.shape[5])
        res = []
        for i in range(2):
            b = 4 * r + 2 * cls + i
            sc = lax.dot_general(q2[:, 0:latent], cacheb[b], (((1,), (1,)), ((), ())), preferred_element_type=jnp.float32)
            sc = sc + jnp.dot(q2[:, latent:latent + rope_dim], ropeb[b], preferred_element_type=jnp.float32)
            groups = []
            for x_ in range(nx):
                for h_ in range(2):
                    k = (h_ * nx + x_) * 16 + 8 * i
                    groups.append(sc[k:k + 8])
            sc = jnp.concatenate(groups, axis=0) * scale
            pos = base + lax.broadcasted_iota(jnp.int32, (n_head, n_pos), 1)
            valid = pos < lens[b]
            sc = jnp.where(valid, sc, NEG_FILL)
            m = jnp.max(sc, axis=1, keepdims=True)
            w = jnp.where(valid, jnp.exp(sc - m), 0.0)
            l = jnp.sum(w, axis=1, keepdims=True)
            acc = jnp.dot(w.astype(jnp.bfloat16), cacheb[b], preferred_element_type=jnp.float32)
            res.append((m, l, acc))
        for x_ in range(nx):
            ml = []
            for g in range(4):
                m, l, acc = res[g // 2]
                k = 16 * x_ + 8 * (g % 2)
                ml.append((m[k:k + 8], l[k:k + 8]))
                for n in range(n_slab):
                    part[cls, r, x_, 32 * n + 8 * g:32 * n + 8 * g + 8, :] = acc[k:k + 8, LANES * n:LANES * n + LANES]
            part[cls, r, x_, 32 * n_slab:32 * n_slab + 8, :] = stats(ml)

    def merge(own, box):
        st, si = own[32 * n_slab:32 * n_slab + 8, :], box[32 * n_slab:32 * n_slab + 8, :]
        ml = []
        for g in range(4):
            m1, m2 = st[:, 32 * g:32 * g + 1], si[:, 32 * g:32 * g + 1]
            l1, l2 = st[:, 32 * g + 16:32 * g + 17], si[:, 32 * g + 16:32 * g + 17]
            m = jnp.maximum(m1, m2)
            e1, e2 = jnp.exp(m1 - m), jnp.exp(m2 - m)
            ml.append((m, l1 * e1 + l2 * e2))
            f1, f2 = jnp.broadcast_to(e1, (8, LANES)), jnp.broadcast_to(e2, (8, LANES))
            for n in range(n_slab):
                k = 32 * n + 8 * g
                own[k:k + 8, :] = own[k:k + 8, :] * f1 + box[k:k + 8, :] * f2
        own[32 * n_slab:32 * n_slab + 8, :] = stats(ml)

    def rs_send(cls, r, x_, i, to):
        send(part.at[cls, r, x_], inbox.at[cls, i], rsend.at[cls, i], rrecv.at[cls, i], to)

    def rs_merge(cls, r, x_, i):
        recv(inbox.at[cls, i], rrecv.at[cls, i])
        merge(part.at[cls, r, x_], inbox.at[cls, i])

    def yy(d):
        return (y + d + ny) % ny

    def a_first(r):
        sg = 1 - 2 * (r % 2)
        rs_send(0, r, xx(2), r, at_x(sg))
        rs_send(0, r, xx(-sg), 4 + 2 * r + (1 + sg) // 2, at_x(-sg))

    def a_second(r):
        sg = 1 - 2 * (r % 2)
        rs_merge(0, r, xx(sg), r)
        rs_send(0, r, xx(sg), 4 + 2 * r + (1 - sg) // 2, at_x(sg))

    def b_send(d, odd):
        for x_ in range(odd, nx, 2):
            rs_send(1, yy(d), x_, 4 + 2 * x_ + (1 - d) // 2, at_y(d))

    def b_second(d, odd):
        for x_ in range(odd, nx, 2):
            rs_merge(1, yy(d), x_, x_)
            rs_send(1, yy(d), x_, 4 + 2 * x_ + (1 - d) // 2, at_y(d))

    def a_final(r):
        for i in range(2):
            rs_merge(0, r, x, 4 + 2 * r + i)

    def b_final(x_):
        for i in range(2):
            rs_merge(1, y, x_, 4 + 2 * x_ + i)

    attend(0, yy(2))
    a_first(yy(2))
    attend(0, yy(1))
    a_first(yy(1))
    attend(0, yy(-1))
    a_first(yy(-1))
    a_second(yy(2))
    attend(0, y)
    a_first(y)
    a_second(yy(1))
    gather_finish(1)
    gather_finish(3)
    attend(1, yy(2))
    for x_ in range(nx):
        rs_send(1, yy(2), x_, x_, at_y(1 - 2 * (x_ % 2)))
    a_second(yy(-1))
    attend(1, yy(1))
    b_send(1, 1)
    a_second(y)
    attend(1, yy(-1))
    b_send(-1, 0)
    b_second(1, 0)
    b_second(-1, 1)
    for d in (2, 1, 3):
        a_final(yy(d))
        rs_send(0, yy(d), x, 11 + d, at_y(d))
    attend(1, y)
    for d in (2, 1, 3):
        b_final(xx(d))
        rs_send(1, y, xx(d), 11 + d, at_x(d))
    a_final(y)
    b_final(x)
    for d in (1, 3, 2):
        rs_merge(0, y, x, 11 + d)
        rs_merge(1, y, x, 11 + d)

    rows = []
    for cls in range(2):
        own = part.at[cls, y, x]
        st = own[32 * n_slab:32 * n_slab + 8, :]
        for g in range(4):
            inv = jnp.broadcast_to(st[:, 32 * g + 16:32 * g + 17], (8, LANES))
            rows.append(jnp.concatenate([own[32 * n + 8 * g:32 * n + 8 * g + 8, :] / inv for n in range(n_slab)], axis=1))
    o_l = jnp.concatenate(rows, axis=0).astype(jnp.bfloat16)
    n_own = o_l.shape[0]
    local[3].wait()
    head_o = lax.broadcasted_iota(jnp.int32, (n_own, wuv.shape[2]), 0) % nh
    v = jnp.zeros((n_own, wuv.shape[2]), jnp.float32)
    for h in range(nh):
        v = jnp.where(head_o == h, jnp.dot(o_l, wuvb[h], preferred_element_type=jnp.float32), v)
    v = v.astype(jnp.bfloat16)
    pi = lax.broadcasted_iota(jnp.int32, (16 * nh, n_own), 0)
    pj = lax.broadcasted_iota(jnp.int32, (16 * nh, n_own), 1)
    perm = jnp.where((pj % nh == pi // 16) & (pj // nh == pi % 16), 1.0, 0.0).astype(jnp.bfloat16)
    vp = jnp.dot(perm, v, preferred_element_type=jnp.float32).astype(jnp.bfloat16)
    lhs = jnp.concatenate([vp[16 * h:16 * h + 16] for h in range(nh)], axis=1)
    local[4].wait()
    n_rows = n_own // nh
    others = [(d, f) for d in (2, 1, 3, 0) for f in (0, 1) if (d, f) != (0, 0)]
    for d, f in others + [(0, 0)]:
        s_ = xx(d) * 2 + (1 - c if f else c)
        piece = jnp.dot(lhs, woutb[:, pl.ds(pl.multiple_of(s_ * cols, LANES), cols)], preferred_element_type=jnp.float32)
        if (d, f) != (0, 0):
            k = 2 * d + f
            k_there = 2 * ((nx - d) % nx) + f
            ybuf[k] = piece[0:n_rows]
            send(ybuf.at[k], yin.at[k_there], ysend.at[k], yrecv.at[k_there], {"ctx": y, "seq": s_})
        else:
            total = piece[0:n_rows]
    for d, f in others:
        recv(yin.at[2 * d + f], yrecv.at[2 * d + f])
        total = total + yin[2 * d + f]
    hid = hidden[:, pl.ds(pl.multiple_of(s * cols, LANES), cols)].astype(jnp.float32)
    mine = hid[0:n_rows]
    for y_ in range(1, ny):
        mine = jnp.where(y == y_, hid[n_rows * y_:n_rows * y_ + n_rows], mine)
    obuf[y * ns + s] = (mine + total).astype(jnp.bfloat16)
    me = y * ns + s
    far = [(e, d, f) for e in (2, 1, 3, 0) for d in (2, 1, 3, 0) for f in (0, 1) if (e, d, f) != (0, 0, 0)]
    far.sort(key=lambda t: -(min(t[0], ny - t[0]) + min(t[1], nx - t[1])))
    for e, d, f in far:
        k = (e * nx + d) * 2 + f
        send(obuf.at[me], obuf.at[me], osend.at[k], orecv.at[k], {"ctx": yy(e), "seq": xx(d) * 2 + (1 - c if f else c)})
    for e, d, f in reversed(far):
        recv(obuf.at[yy(-e) * ns + xx(-d) * 2 + (1 - c if f else c)], orecv.at[(e * nx + d) * 2 + f])
    for s_ in range(ns):
        out[:, s_ * cols:(s_ + 1) * cols] = jnp.concatenate(
            [obuf[y_ * ns + s_].astype(jnp.float32) for y_ in range(ny)], axis=0).astype(jnp.bfloat16)
    for copy in sends:
        copy.wait_send()
    for copy in swap:
        copy.wait_send()


def solution(mesh):
    ny, ns = mesh.shape['ctx'], mesh.shape['seq']
    row_spec = P('batch', None)
    cache_spec = P('batch', ('ctx', 'seq'), None)
    proj_spec = P(None, 'seq', None)
    head_spec = P('seq', None, None)

    def local_step(hidden, lengths, latent_cache, rope_keys, w_uq, w_qr, w_uk, w_uv, w_out):
        rope_t = jnp.transpose(rope_keys, (0, 2, 1))
        nb, d_model = hidden.shape
        t_own, latent = latent_cache.shape[1:]
        nh = w_uq.shape[1]
        wqr_t = jnp.transpose(w_qr, (1, 2, 0))
        rope_dim = rope_t.shape[1]
        nx = ns // 2
        cols = d_model // ns
        n_rows = nb // ny
        bf, f32 = jnp.bfloat16, jnp.float32
        unit = (latent // LANES) * 32 + 8
        wide = latent + LANES
        dma = pltpu.SemaphoreType.DMA
        vmem = pl.BlockSpec(memory_space=pltpu.VMEM)
        anyw = pl.BlockSpec(memory_space=pl.ANY)
        import functools
        out = pl.pallas_call(
            functools.partial(decode_kernel, ny, ns),
            out_shape=jax.ShapeDtypeStruct(hidden.shape, bf),
            in_specs=[pl.BlockSpec(memory_space=pltpu.SMEM), vmem, anyw, anyw, anyw, anyw, anyw, anyw, anyw],
            out_specs=vmem,
            scratch_shapes=[
                pltpu.VMEM((nb, 2 * t_own, latent), bf),
                pltpu.VMEM((nb, rope_dim, 2 * t_own), bf),
                pltpu.VMEM((2, nb // 4, 2, nx, 16, wide), bf),
                pltpu.VMEM((2, ny, nx, unit, LANES), f32),
                pltpu.VMEM((2, 15, unit, LANES), f32),
                pltpu.VMEM((nh // 2,) + w_uk.shape[1:], bf),
                pltpu.VMEM(w_uv.shape, bf),
                pltpu.VMEM((w_out.shape[0] * w_out.shape[1], d_model), bf),
                pltpu.VMEM((d_model, nh // 2, w_uq.shape[2]), bf),
                pltpu.VMEM((nh // 2, rope_dim, d_model), bf),
                pltpu.VMEM((d_model // 256 * 16, 256 * nh // 2), bf),
                pltpu.VMEM((ns, n_rows, cols), f32),
                pltpu.VMEM((ns, n_rows, cols), f32),
                pltpu.VMEM((ny * ns, n_rows, cols), bf),
                dma((5,)), dma((d_model // 256,)), dma((nh // 4,)), dma((2,)), dma((2,)), dma((4, 5, 4)), dma((4, 5, 4)), dma((2, 15)), dma((2, 15)),
                dma((ns,)), dma((ns,)), dma((ny * ns,)), dma((ny * ns,)),
            ],
            compiler_params=pltpu.CompilerParams(collective_id=0, has_side_effects=True, vmem_limit_bytes=60 * 2 ** 20),
        )(lengths, hidden, w_uq.reshape(d_model, 2, nh // 2, -1), wqr_t, w_uk, latent_cache, rope_t, w_uv, w_out.reshape(-1, d_model))
        return out

    return jax.shard_map(local_step, mesh=mesh,
                         in_specs=(row_spec, P('batch'), cache_spec, cache_spec, proj_spec, proj_spec, head_spec, head_spec, head_spec),
                         out_specs=row_spec, check_vma=False)
```

time: 85.4 us -> 67.5 us (0.79)
  matrix products: 14.4 us -> 0 us
  Pallas kernels: 67.9 us -> 65.8 us
  local copies, waits for them, and re-layouts: 2.93 us -> 1.59 us
    dot_general x2 -> x0, matrix products: 14.4 us -> none  [the longest x1 10.2 us: local_step(): jnp.einsum('bd,dhk->bhk', hidden, w_uq, preferred_element_type=jnp.float32)]
    pallas_call x1, Pallas kernels: 67.9 us -> 65.8 us  [local_step(): pl.pallas_call(functools.partial(decode_kernel, ny, ns), out_shape=jax.Sh...]
    dot_general x2 -> x0, local copies, waits for them, and re-layouts: 1.3 us -> none  [the longest x1 0.65 us: local_step(): jnp.einsum('bd,dhk->bhk', hidden, w_uq, preferred_element_type=jnp.float32)]
    transpose x1 -> x0, local copies, waits for them, and re-layouts: 0.94 us -> none  [local_step(): return jnp.transpose(out, (0, 2, 1, 3)).reshape(nb, d_model)]
    unnamed x5 -> x1, local copies, waits for them, and re-layouts: 0.69 us -> 1.59 us
where the time goes in v2:
time: 67.5 us; the launch traced here: 67.4 us
  Pallas kernels  65.8 us (97%)
  local copies, waits for them, and re-layouts  1.59 us (2%)
    pallas_call x1, Pallas kernels, local_step(): pl.pallas_call(functools.partial(decode_kernel, ny, ns), out_shape=jax.Sh...  65.8 us
    unnamed x1, local copies, waits for them, and re-layouts  1.59 us

profile of v2, /device:TPU:97, one launch (start us, length us, event | category | flops | bytes accessed | tf_op | source)
XLA Modules:
  0.0 67.4 jit_solution(7180333147162665849)
XLA Ops:
  0.0 65.8 %shard_map.91 = bf16[16,5120]{1,0:T(8,128)(2,1)} custom-call(s32[16]{0:T(128)} %lens.1, bf16[16,5120]{1,0:T(8,128)(2,1)} %hidden.1, bf16[5120,2,8,128]{3,2,1,0:T(8,128)(2,1)} %bitcast.4, bf16[16,64,5120]{2,1,0:T(8,128)(2,1)} %bitcast.6, bf16[16,128,512]{2,1,0:T(8,128)(2,1)} %wuk.1, bf16[16,256,512]{2,1,0:T(8,128)(2,1)} %cache.1, ...), custom_call_target="tpu_custom_call" | custom-call | tf_op jit(solution)/shard_map/pallas_call | solution.py:391
  65.8 1.6 %copy.11 = bf16[16,5120]{1,0:T(8,128)(2,1)} copy(bf16[16,5120]{1,0:T(8,128)(2,1)} %shard_map.91) | data formatting | bytes 327680

commit v3 on v2

--- a/solution.py
+++ b/solution.py
@@ -5,7 +5,8 @@
 from jax.experimental.pallas import tpu as pltpu
 from jax.sharding import PartitionSpec as P
 
-NEG_FILL = -1.0e30
+NEG_FILL = -3.0e38
+MAX_FLOOR = -1.5e38
 LANES = 128
 MESH = pl.DeviceIdType.MESH
 
@@ -46,12 +47,18 @@
     span = pl.ds(c * t_own, t_own)
     local = [
         pltpu.make_async_copy(wuk.at[pl.ds(hb * half_h, half_h)], wukb, lsem.at[0]),
-        pltpu.make_async_copy(cache, cacheb.at[:, span], lsem.at[1]),
+        pltpu.make_async_copy(cache, cacheb.at[:, span, pl.ds(0, latent)], lsem.at[1]),
         pltpu.make_async_copy(rope, ropeb.at[:, :, span], lsem.at[2]),
         pltpu.make_async_copy(wuv, wuvb, lsem.at[3]),
         pltpu.make_async_copy(wout, woutb, lsem.at[4]),
     ]
-    for copy in qr + uq:
+    loads = []
+    for k in range(n_step // group):
+        if k < half_h // r_step:
+            loads.append((1, k, qr[k]))
+        loads.append((0, k, uq[k]))
+    in_flight = 5
+    for _, _, copy in loads[:in_flight]:
         copy.start()
 
     barrier = pltpu.get_barrier_semaphore()
@@ -78,33 +85,37 @@
     mate = {"ctx": y, "seq": s + 1 - 2 * c}
     other = pl.ds((1 - c) * t_own, t_own)
     swap = [
-        pltpu.make_async_remote_copy(cache, cacheb.at[:, span], csend.at[0], crecv.at[0], device_id=mate, device_id_type=MESH),
+        pltpu.make_async_remote_copy(cache, cacheb.at[:, span, pl.ds(0, latent)], csend.at[0], crecv.at[0], device_id=mate, device_id_type=MESH),
         pltpu.make_async_remote_copy(rope, ropeb.at[:, :, span], csend.at[1], crecv.at[1], device_id=mate, device_id_type=MESH),
     ]
-    for copy in swap:
-        copy.start()
-
     q_rope = []
-    for copy in qr:
-        copy.wait()
-    for k in range(half_h // r_step):
-        w = wqrb[k * r_step:(k + 1) * r_step].reshape(r_step * rope_dim, d_model)
-        q_rope.append(lax.dot_general(w, hid2, (((1,), (1,)), ((), ())), preferred_element_type=jnp.float32))
-    q_rope = jnp.concatenate(q_rope, axis=0).T
-    q_rope = jnp.concatenate([q_rope[0:half_b, rope_dim * h:rope_dim * (h + 1)] for h in range(half_h)], axis=0).astype(jnp.bfloat16)
     lane_h = lax.broadcasted_iota(jnp.int32, (2 * half_b, wide_k), 1) % half_h
     row_h = lax.broadcasted_iota(jnp.int32, (2 * half_b, wide_k), 0) // half_b
     sums = [jnp.zeros((half_h * half_b, nope), jnp.float32) for _ in range(2)]
-    for g in range(n_step // group):
-        uq[g].wait()
-        for k in range(g * group, (g + 1) * group):
-            hr = hrep[2 * half_b * k:2 * half_b * (k + 1), :]
-            lhs = jnp.concatenate([jnp.where(lane_h == row_h + h, hr, jnp.zeros_like(hr)) for h in range(0, half_h, 2)], axis=0)
-            w = wuqb[k * step:(k + 1) * step].reshape(wide_k, nope)
-            sums[k % 2] = sums[k % 2] + jnp.dot(lhs, w, preferred_element_type=jnp.float32)
-        if g == 2:
-            for copy in local[:3]:
-                copy.start()
+    for i, (kind, n, copy) in enumerate(loads):
+        copy.wait()
+        if i + in_flight < len(loads):
+            loads[i + in_flight][2].start()
+        else:
+            k = i + in_flight - len(loads)
+            if k < 3:
+                local[k].start()
+        if i == 5:
+            for swap_copy in reversed(swap):
+                swap_copy.start()
+        if kind == 1:
+            half = r_step * rope_dim // 2
+            w = wqrb[n * r_step:(n + 1) * r_step].reshape(r_step * rope_dim, d_model)
+            for p in range(2):
+                q_rope.append(lax.dot_general(w[half * p:half * p + half], hid2, (((1,), (1,)), ((), ())), preferred_element_type=jnp.float32))
+        else:
+            for k in range(n * group, (n + 1) * group):
+                hr = hrep[2 * half_b * k:2 * half_b * (k + 1), :]
+                lhs = jnp.concatenate([jnp.where(lane_h == row_h + h, hr, jnp.zeros_like(hr)) for h in range(0, half_h, 2)], axis=0)
+                w = wuqb[k * step:(k + 1) * step].reshape(wide_k, nope)
+                sums[k % 2] = sums[k % 2] + jnp.dot(lhs, w, preferred_element_type=jnp.float32)
+    q_rope = jnp.concatenate(q_rope, axis=0).T
+    q_rope = jnp.concatenate([q_rope[0:half_b, rope_dim * h:rope_dim * (h + 1)] for h in range(half_h)], axis=0).astype(jnp.bfloat16)
     q_nope = (sums[0] + sums[1]).astype(jnp.bfloat16)
 
     n_q = half_b * half_h
@@ -168,8 +179,11 @@
         copy.start()
     for copy in local[1:3]:
         copy.wait()
-    recv(cacheb.at[:, other], crecv.at[0])
+    recv(cacheb.at[:, other, pl.ds(0, latent)], crecv.at[0])
     recv(ropeb.at[:, :, other], crecv.at[1])
+    for b in range(nb):
+        keys = jnp.concatenate([ropeb[b], jnp.zeros((LANES - rope_dim, n_pos), jnp.bfloat16)], axis=0)
+        cacheb[b, :, latent:] = keys.T
     gather_finish(0)
     gather_finish(2)
 
@@ -185,60 +199,74 @@
             tile = jnp.where((lane >= 32 * i + 16) & (lane < 32 * i + 32), l_, tile)
         return tile
 
-    def attend(cls, r):
-        j = cls + 2 * (r % 2)
-        r_ = r // 2
-        q2 = qbuf[r_, j].reshape(2 * n_head, qbuf.shape[5])
+    def attend(*pairs):
+        first = lax.broadcasted_iota(jnp.int32, (n_pos, 2 * n_head), 1) % 16 < 8
+        first_row = lax.broadcasted_iota(jnp.int32, (1, 2 * n_head), 1) % 16 < 8
+        pos = lax.broadcasted_iota(jnp.int32, (n_pos, 2 * n_head), 0)
+        b0s = [4 * r + 2 * (1 - cls) for cls, r in pairs]
+        scores = []
+        for (cls, r), b0 in zip(pairs, b0s):
+            q2 = qbuf[r // 2, 1 - cls + 2 * (r % 2)].reshape(2 * n_head, qbuf.shape[5])
+            scores.append([lax.dot_general(cacheb[b0 + i], q2, (((1,), (1,)), ((), ())), preferred_element_type=jnp.float32) for i in range(2)])
         res = []
-        for i in range(2):
-            b = 4 * r + 2 * cls + i
-            sc = lax.dot_general(q2[:, 0:latent], cacheb[b], (((1,), (1,)), ((), ())), preferred_element_type=jnp.float32)
-            sc = sc + jnp.dot(q2[:, latent:latent + rope_dim], ropeb[b], preferred_element_type=jnp.float32)
-            groups = []
+        for sc, b0 in zip(scores, b0s):
+            limit = jnp.where(first_row, lens[b0], lens[b0 + 1]) - base
+            sc = jnp.where(first, sc[0], sc[1]) * scale
+            sc = jnp.where(pos < limit, sc, NEG_FILL)
+            m = jnp.maximum(jnp.max(sc, axis=0, keepdims=True), MAX_FLOOR)
+            w = jnp.exp(sc - m)
+            l = jnp.sum(w, axis=0, keepdims=True)
+            res.append((m, l, w.astype(jnp.bfloat16).T))
+        new = []
+        for (m, l, w), b0 in zip(res, b0s):
+            acc = [jnp.dot(w, cacheb[b0 + i, :, 0:latent], preferred_element_type=jnp.float32) for i in range(2)]
+            new.append((acc, jnp.concatenate([m, l, jnp.zeros((6, 2 * n_head), jnp.float32)], axis=0).T))
+        for (cls, r), (acc, ml_cols) in zip(pairs, new):
             for x_ in range(nx):
-                for h_ in range(2):
-                    k = (h_ * nx + x_) * 16 + 8 * i
-                    groups.append(sc[k:k + 8])
-            sc = jnp.concatenate(groups, axis=0) * scale
-            pos = base + lax.broadcasted_iota(jnp.int32, (n_head, n_pos), 1)
-            valid = pos < lens[b]
-            sc = jnp.where(valid, sc, NEG_FILL)
-            m = jnp.max(sc, axis=1, keepdims=True)
-            w = jnp.where(valid, jnp.exp(sc - m), 0.0)
-            l = jnp.sum(w, axis=1, keepdims=True)
-            acc = jnp.dot(w.astype(jnp.bfloat16), cacheb[b], preferred_element_type=jnp.float32)
-            res.append((m, l, acc))
-        for x_ in range(nx):
+                ml = []
+                for g in range(4):
+                    k = ((g % 2) * nx + x_) * 16 + 8 * (g // 2)
+                    ml.append((ml_cols[k:k + 8, 0:1], ml_cols[k:k + 8, 1:2]))
+                    for n in range(n_slab):
+                        part[cls, r, x_, 32 * n + 8 * g:32 * n + 8 * g + 8, :] = acc[g // 2][k:k + 8, LANES * n:LANES * n + LANES]
+                part[cls, r, x_, 32 * n_slab:32 * n_slab + 8, :] = stats(ml)
+
+    def merge(items):
+        new = []
+        row = 32 * n_slab
+        for own, boxes in items:
+            refs = [own] + boxes
+            tiles = [ref[row:row + 8, :] for ref in refs]
             ml = []
             for g in range(4):
-                m, l, acc = res[g // 2]
-                k = 16 * x_ + 8 * (g % 2)
-                ml.append((m[k:k + 8], l[k:k + 8]))
+                ms = [jnp.broadcast_to(t[:, 32 * g:32 * g + 1], (8, LANES)) for t in tiles]
+                ls = [jnp.broadcast_to(t[:, 32 * g + 16:32 * g + 17], (8, LANES)) for t in tiles]
+                m = ms[0]
+                for other_m in ms[1:]:
+                    m = jnp.maximum(m, other_m)
+                es = [jnp.exp(m_ - m) for m_ in ms]
+                l = ls[0] * es[0]
+                for l_, e_ in zip(ls[1:], es[1:]):
+                    l = l + l_ * e_
+                ml.append((m, l))
                 for n in range(n_slab):
-                    part[cls, r, x_, 32 * n + 8 * g:32 * n + 8 * g + 8, :] = acc[k:k + 8, LANES * n:LANES * n + LANES]
-            part[cls, r, x_, 32 * n_slab:32 * n_slab + 8, :] = stats(ml)
-
-    def merge(own, box):
-        st, si = own[32 * n_slab:32 * n_slab + 8, :], box[32 * n_slab:32 * n_slab + 8, :]
-        ml = []
-        for g in range(4):
-            m1, m2 = st[:, 32 * g:32 * g + 1], si[:, 32 * g:32 * g + 1]
-            l1, l2 = st[:, 32 * g + 16:32 * g + 17], si[:, 32 * g + 16:32 * g + 17]
-            m = jnp.maximum(m1, m2)
-            e1, e2 = jnp.exp(m1 - m), jnp.exp(m2 - m)
-            ml.append((m, l1 * e1 + l2 * e2))
-            f1, f2 = jnp.broadcast_to(e1, (8, LANES)), jnp.broadcast_to(e2, (8, LANES))
-            for n in range(n_slab):
-                k = 32 * n + 8 * g
-                own[k:k + 8, :] = own[k:k + 8, :] * f1 + box[k:k + 8, :] * f2
-        own[32 * n_slab:32 * n_slab + 8, :] = stats(ml)
+                    k = 32 * n + 8 * g
+                    total = refs[0][k:k + 8, :] * es[0]
+                    for ref, e_ in zip(refs[1:], es[1:]):
+                        total = total + ref[k:k + 8, :] * e_
+                    new.append((own, k, total))
+            new.append((own, row, stats(ml)))
+        for own, k, value in new:
+            own[k:k + 8, :] = value
 
     def rs_send(cls, r, x_, i, to):
         send(part.at[cls, r, x_], inbox.at[cls, i], rsend.at[cls, i], rrecv.at[cls, i], to)
 
-    def rs_merge(cls, r, x_, i):
-        recv(inbox.at[cls, i], rrecv.at[cls, i])
-        merge(part.at[cls, r, x_], inbox.at[cls, i])
+    def rs_merge(*items):
+        for cls, _, _, slots in items:
+            for i in slots:
+                recv(inbox.at[cls, i], rrecv.at[cls, i])
+        merge([(part.at[cls, r, x_], [inbox.at[cls, i] for i in slots]) for cls, r, x_, slots in items])
 
     def yy(d):
         return (y + d + ny) % ny
@@ -250,7 +278,7 @@
 
     def a_second(r):
         sg = 1 - 2 * (r % 2)
-        rs_merge(0, r, xx(sg), r)
+        rs_merge((0, r, xx(sg), [r]))
         rs_send(0, r, xx(sg), 4 + 2 * r + (1 - sg) // 2, at_x(sg))
 
     def b_send(d, odd):
@@ -258,56 +286,42 @@
             rs_send(1, yy(d), x_, 4 + 2 * x_ + (1 - d) // 2, at_y(d))
 
     def b_second(d, odd):
+        rs_merge(*[(1, yy(d), x_, [x_]) for x_ in range(odd, nx, 2)])
         for x_ in range(odd, nx, 2):
-            rs_merge(1, yy(d), x_, x_)
             rs_send(1, yy(d), x_, 4 + 2 * x_ + (1 - d) // 2, at_y(d))
 
-    def a_final(r):
-        for i in range(2):
-            rs_merge(0, r, x, 4 + 2 * r + i)
-
-    def b_final(x_):
-        for i in range(2):
-            rs_merge(1, y, x_, 4 + 2 * x_ + i)
-
-    attend(0, yy(2))
-    a_first(yy(2))
-    attend(0, yy(1))
-    a_first(yy(1))
-    attend(0, yy(-1))
-    a_first(yy(-1))
-    a_second(yy(2))
-    attend(0, y)
-    a_first(y)
-    a_second(yy(1))
+    def pair(r):
+        return [4 + 2 * r, 5 + 2 * r]
+
+    attend((1, yy(2)), (1, yy(1)))
+    for x_ in range(nx):
+        rs_send(1, yy(2), x_, x_, at_y(1 - 2 * (x_ % 2)))
+    b_send(1, 1)
     gather_finish(1)
     gather_finish(3)
-    attend(1, yy(2))
-    for x_ in range(nx):
-        rs_send(1, yy(2), x_, x_, at_y(1 - 2 * (x_ % 2)))
-    a_second(yy(-1))
-    attend(1, yy(1))
-    b_send(1, 1)
-    a_second(y)
-    attend(1, yy(-1))
+    attend((0, yy(2)), (1, yy(-1)))
+    a_first(yy(2))
     b_send(-1, 0)
+    attend((0, yy(1)), (0, yy(-1)))
+    a_first(yy(1))
+    a_first(yy(-1))
+    attend((0, y), (1, y))
+    a_first(y)
     b_second(1, 0)
     b_second(-1, 1)
+    a_second(yy(2))
+    a_second(yy(1))
+    a_second(yy(-1))
+    a_second(y)
     for d in (2, 1, 3):
-        a_final(yy(d))
+        rs_merge((0, yy(d), x, pair(yy(d))), (1, y, xx(d), pair(xx(d))))
         rs_send(0, yy(d), x, 11 + d, at_y(d))
-    attend(1, y)
-    for d in (2, 1, 3):
-        b_final(xx(d))
         rs_send(1, y, xx(d), 11 + d, at_x(d))
-    a_final(y)
-    b_final(x)
-    for d in (1, 3, 2):
-        rs_merge(0, y, x, 11 + d)
-        rs_merge(1, y, x, 11 + d)
+    rs_merge((0, y, x, pair(y)), (1, y, x, pair(x)))
+    rs_merge((0, y, x, [12, 13, 14]), (1, y, x, [12, 13, 14]))
 
     rows = []
-    for cls in range(2):
+    for cls in (1, 0):
         own = part.at[cls, y, x]
         st = own[32 * n_slab:32 * n_slab + 8, :]
         for g in range(4):
@@ -394,7 +408,7 @@
             in_specs=[pl.BlockSpec(memory_space=pltpu.SMEM), vmem, anyw, anyw, anyw, anyw, anyw, anyw, anyw],
             out_specs=vmem,
             scratch_shapes=[
-                pltpu.VMEM((nb, 2 * t_own, latent), bf),
+                pltpu.VMEM((nb, 2 * t_own, wide), bf),
                 pltpu.VMEM((nb, rope_dim, 2 * t_own), bf),
                 pltpu.VMEM((2, nb // 4, 2, nx, 16, wide), bf),
                 pltpu.VMEM((2, ny, nx, unit, LANES), f32),

time: 67.5 us -> 60.1 us (0.89)
  Pallas kernels: 65.8 us -> 58.4 us
    pallas_call x1, Pallas kernels: 65.8 us -> 58.4 us  [local_step(): pl.pallas_call(functools.partial(decode_kernel, ny, ns), out_shape=jax.Sh...]
where the time goes in v3:
time: 60.1 us; the launch traced here: 60 us
  Pallas kernels  58.4 us (97%)
  local copies, waits for them, and re-layouts  1.59 us (3%)
    pallas_call x1, Pallas kernels, local_step(): pl.pallas_call(functools.partial(decode_kernel, ny, ns), out_shape=jax.Sh...  58.4 us
    unnamed x1, local copies, waits for them, and re-layouts  1.59 us

profile of v3, /device:TPU:97, one launch (start us, length us, event | category | flops | bytes accessed | tf_op | source)
XLA Modules:
  0.0 60.0 jit_solution(7112182878074211087)
XLA Ops:
  0.0 58.4 %shard_map.91 = bf16[16,5120]{1,0:T(8,128)(2,1)} custom-call(s32[16]{0:T(128)} %lens.1, bf16[16,5120]{1,0:T(8,128)(2,1)} %hidden.1, bf16[5120,2,8,128]{3,2,1,0:T(8,128)(2,1)} %bitcast.4, bf16[16,64,5120]{2,1,0:T(8,128)(2,1)} %bitcast.6, bf16[16,128,512]{2,1,0:T(8,128)(2,1)} %wuk.1, bf16[16,256,512]{2,1,0:T(8,128)(2,1)} %cache.1, ...), custom_call_target="tpu_custom_call" | custom-call | tf_op jit(solution)/shard_map/pallas_call | solution.py:405
  58.4 1.6 %copy.11 = bf16[16,5120]{1,0:T(8,128)(2,1)} copy(bf16[16,5120]{1,0:T(8,128)(2,1)} %shard_map.91) | data formatting | bytes 327680

commit v4 on v3

--- a/solution.py
+++ b/solution.py
@@ -11,9 +11,9 @@
 MESH = pl.DeviceIdType.MESH
 
 
-def decode_kernel(ny, ns, lens, hidden, wuq, wqr, wuk, cache, rope, wuv, wout, out,
-                  cacheb, ropeb, qbuf, part, inbox, wukb, wuvb, woutb, wuqb, wqrb, hrep, ybuf, yin, obuf,
-                  lsem, usem, qsem, csend, crecv, gsend, grecv, rsend, rrecv, ysend, yrecv, osend, orecv):
+def decode_kernel(ny, ns, lens_in, hidden_in, wuq, wqr, wuk, cache, rope, wuv, wout, out,
+                  lens, hidden, cacheb, ropeb, qbuf, part, inbox, wukb, wuvb, woutb, wuqb, wqrb, hrep, ybuf, yin, obuf,
+                  lsem, usem, qsem, csend, crecv, gsend, grecv, rsend, rrecv, tail_sem):
     nx = ns // 2
     y, s = lax.axis_index("ctx"), lax.axis_index("seq")
     x, c = s // 2, s % 2
@@ -58,6 +58,9 @@
             loads.append((1, k, qr[k]))
         loads.append((0, k, uq[k]))
     in_flight = 5
+    small = [pltpu.make_async_copy(hidden_in, hidden, lsem.at[5]), pltpu.make_async_copy(lens_in, lens, lsem.at[6])]
+    for copy in small:
+        copy.start()
     for _, _, copy in loads[:in_flight]:
         copy.start()
 
@@ -68,6 +71,8 @@
                 pl.semaphore_signal(barrier, inc=1, device_id={"ctx": (y + dy) % ny, "seq": (s + ds) % ns},
                                     device_id_type=MESH)
 
+    for copy in small:
+        copy.wait()
     wide_k = step * half_h
     si = lax.broadcasted_iota(jnp.int32, (2 * half_b, nb), 0)
     sj = lax.broadcasted_iota(jnp.int32, (2 * half_b, nb), 1)
@@ -123,25 +128,27 @@
     qj = lax.broadcasted_iota(jnp.int32, (n_q, n_q), 1)
     pick = jnp.where((qi % half_h == qj // half_b) & (qi // half_h == qj % half_b), 1.0, 0.0).astype(jnp.bfloat16)
     q_nope = jnp.dot(pick, q_nope, preferred_element_type=jnp.float32).astype(jnp.bfloat16)
-    q_rope = jnp.dot(pick, q_rope, preferred_element_type=jnp.float32).astype(jnp.bfloat16)
+    q_rope = jnp.dot(pick, q_rope, preferred_element_type=jnp.float32)
     head_of = lax.broadcasted_iota(jnp.int32, (n_q, nope), 0) % half_h
     big = jnp.concatenate([jnp.where(head_of == h, q_nope, jnp.zeros_like(q_nope)) for h in range(half_h)], axis=1)
     local[0].wait()
     q_lat = jnp.dot(big, wukb[...].reshape(half_h * nope, latent), preferred_element_type=jnp.float32).astype(jnp.bfloat16)
-    q_rope = jnp.concatenate([q_rope, jnp.zeros((n_q, LANES - rope_dim), jnp.bfloat16)], axis=1)
     for j in range(half_b // 2):
-        qbuf[rb, j, hb, x, :, 0:latent] = q_lat[16 * j:16 * j + 16]
-        qbuf[rb, j, hb, x, :, latent:] = q_rope[16 * j:16 * j + 16]
-
-    sends = []
+        for n in range(latent // LANES):
+            qbuf[rb, j, hb, x, 16 * n:16 * n + 16, :] = q_lat[16 * j:16 * j + 16, LANES * n:LANES * n + LANES]
+        sides = [q_rope[16 * j + 8 * i:16 * j + 8 * i + 8] for i in range(2)]
+        qbuf[rb, j, hb, x, 64:72, :] = jnp.concatenate(sides, axis=1).astype(jnp.bfloat16)
+
 
     def send(src, dst, ssem, rsem, to):
         copy = pltpu.make_async_remote_copy(src, dst, ssem, rsem, device_id=to, device_id_type=MESH)
         copy.start()
-        sends.append(copy)
 
     def recv(dst, rsem):
         pltpu.make_async_remote_copy(dst, dst, rsem, rsem, device_id=mate, device_id_type=MESH).wait_recv()
+
+    def sent(src, ssem):
+        pltpu.make_async_remote_copy(src, src, ssem, ssem, device_id=mate, device_id_type=MESH).wait_send()
 
     def rbhb(d):
         yy = (y + d + ny) % ny
@@ -157,7 +164,7 @@
 
     def hop(j, stage, ref, along_x):
         for d in (2, 1, 3):
-            send(ref, ref, gsend.at[j, stage, d], grecv.at[j, stage, d], at_x(d) if along_x else at_y(d))
+            send(ref, ref, gsend.at[1 if stage else 0], grecv.at[j, 0 if stage else d], at_x(d) if along_x else at_y(d))
 
     for a in range(2):
         for j in (a, a + 2):
@@ -167,13 +174,11 @@
     for a in range(2):
         for e in (1, 3, 2):
             for j in (a, a + 2):
-                recv(cell(j, e, 0), grecv.at[j, 0, e])
+                recv(cell(j, e, 0), grecv.at[j, e])
                 hop(j, 1 + e, cell(j, e, 0), j >= 2)
 
     def gather_finish(j):
-        for e in range(4):
-            for d in (1, 3, 2):
-                recv(cell(j, e, d), grecv.at[j, 1 + e, d])
+        recv(qbuf.at[0, 0:3, 0], grecv.at[j, 0])
 
     for copy in local[3:]:
         copy.start()
@@ -182,7 +187,8 @@
     recv(cacheb.at[:, other, pl.ds(0, latent)], crecv.at[0])
     recv(ropeb.at[:, :, other], crecv.at[1])
     for b in range(nb):
-        keys = jnp.concatenate([ropeb[b], jnp.zeros((LANES - rope_dim, n_pos), jnp.bfloat16)], axis=0)
+        blank = jnp.zeros((LANES - rope_dim, n_pos), jnp.bfloat16)
+        keys = jnp.concatenate([blank, ropeb[b]] if b % 2 else [ropeb[b], blank], axis=0)
         cacheb[b, :, latent:] = keys.T
     gather_finish(0)
     gather_finish(2)
@@ -206,7 +212,11 @@
         b0s = [4 * r + 2 * (1 - cls) for cls, r in pairs]
         scores = []
         for (cls, r), b0 in zip(pairs, b0s):
-            q2 = qbuf[r // 2, 1 - cls + 2 * (r % 2)].reshape(2 * n_head, qbuf.shape[5])
+            r_, j_ = r // 2, 1 - cls + 2 * (r % 2)
+            slabs = [qbuf[r_, j_, :, :, 16 * n:16 * n + 16, :].reshape(2 * n_head, LANES) for n in range(n_slab)]
+            side = qbuf[r_, j_, :, :, 64:72, :]
+            side = jnp.concatenate([side, side], axis=2).reshape(2 * n_head, LANES)
+            q2 = jnp.concatenate(slabs + [side], axis=1)
             scores.append([lax.dot_general(cacheb[b0 + i], q2, (((1,), (1,)), ((), ())), preferred_element_type=jnp.float32) for i in range(2)])
         res = []
         for sc, b0 in zip(scores, b0s):
@@ -259,43 +269,42 @@
         for own, k, value in new:
             own[k:k + 8, :] = value
 
-    def rs_send(cls, r, x_, i, to):
-        send(part.at[cls, r, x_], inbox.at[cls, i], rsend.at[cls, i], rrecv.at[cls, i], to)
+    def rs_send(cls, r, x_, i, sem, to):
+        send(part.at[cls, r, x_], inbox.at[cls, i], rsend.at[0], rrecv.at[cls, sem], to)
 
     def rs_merge(*items):
-        for cls, _, _, slots in items:
-            for i in slots:
-                recv(inbox.at[cls, i], rrecv.at[cls, i])
-        merge([(part.at[cls, r, x_], [inbox.at[cls, i] for i in slots]) for cls, r, x_, slots in items])
+        for cls, _, _, i, n, sem in items:
+            recv(inbox.at[cls, pl.ds(i, n)], rrecv.at[cls, sem])
+        merge([(part.at[cls, r, x_], [inbox.at[cls, i + k] for k in range(n)]) for cls, r, x_, i, n, _ in items])
 
     def yy(d):
         return (y + d + ny) % ny
 
     def a_first(r):
         sg = 1 - 2 * (r % 2)
-        rs_send(0, r, xx(2), r, at_x(sg))
-        rs_send(0, r, xx(-sg), 4 + 2 * r + (1 + sg) // 2, at_x(-sg))
+        rs_send(0, r, xx(2), r, r, at_x(sg))
+        rs_send(0, r, xx(-sg), 4 + 2 * r + (1 + sg) // 2, 4 + r, at_x(-sg))
 
     def a_second(r):
         sg = 1 - 2 * (r % 2)
-        rs_merge((0, r, xx(sg), [r]))
-        rs_send(0, r, xx(sg), 4 + 2 * r + (1 - sg) // 2, at_x(sg))
+        rs_merge((0, r, xx(sg), r, 1, r))
+        rs_send(0, r, xx(sg), 4 + 2 * r + (1 - sg) // 2, 4 + r, at_x(sg))
 
     def b_send(d, odd):
         for x_ in range(odd, nx, 2):
-            rs_send(1, yy(d), x_, 4 + 2 * x_ + (1 - d) // 2, at_y(d))
+            rs_send(1, yy(d), x_, 4 + 2 * x_ + (1 - d) // 2, 4 + x_, at_y(d))
 
     def b_second(d, odd):
-        rs_merge(*[(1, yy(d), x_, [x_]) for x_ in range(odd, nx, 2)])
+        rs_merge(*[(1, yy(d), x_, x_, 1, x_) for x_ in range(odd, nx, 2)])
         for x_ in range(odd, nx, 2):
-            rs_send(1, yy(d), x_, 4 + 2 * x_ + (1 - d) // 2, at_y(d))
-
-    def pair(r):
-        return [4 + 2 * r, 5 + 2 * r]
+            rs_send(1, yy(d), x_, 4 + 2 * x_ + (1 - d) // 2, 4 + x_, at_y(d))
+
+    def pair(cls, r, x_, k):
+        return (cls, r, x_, 4 + 2 * k, 2, 4 + k)
 
     attend((1, yy(2)), (1, yy(1)))
     for x_ in range(nx):
-        rs_send(1, yy(2), x_, x_, at_y(1 - 2 * (x_ % 2)))
+        rs_send(1, yy(2), x_, x_, x_, at_y(1 - 2 * (x_ % 2)))
     b_send(1, 1)
     gather_finish(1)
     gather_finish(3)
@@ -314,11 +323,11 @@
     a_second(yy(-1))
     a_second(y)
     for d in (2, 1, 3):
-        rs_merge((0, yy(d), x, pair(yy(d))), (1, y, xx(d), pair(xx(d))))
-        rs_send(0, yy(d), x, 11 + d, at_y(d))
-        rs_send(1, y, xx(d), 11 + d, at_x(d))
-    rs_merge((0, y, x, pair(y)), (1, y, x, pair(x)))
-    rs_merge((0, y, x, [12, 13, 14]), (1, y, x, [12, 13, 14]))
+        rs_merge(pair(0, yy(d), x, yy(d)), pair(1, y, xx(d), xx(d)))
+        rs_send(0, yy(d), x, 11 + d, 8, at_y(d))
+        rs_send(1, y, xx(d), 11 + d, 8, at_x(d))
+    rs_merge(pair(0, y, x, y), pair(1, y, x, x))
+    rs_merge((0, y, x, 12, 3, 8), (1, y, x, 12, 3, 8))
 
     rows = []
     for cls in (1, 0):
@@ -350,11 +359,11 @@
             k = 2 * d + f
             k_there = 2 * ((nx - d) % nx) + f
             ybuf[k] = piece[0:n_rows]
-            send(ybuf.at[k], yin.at[k_there], ysend.at[k], yrecv.at[k_there], {"ctx": y, "seq": s_})
+            send(ybuf.at[k], yin.at[k_there], tail_sem.at[0], tail_sem.at[1], {"ctx": y, "seq": s_})
         else:
             total = piece[0:n_rows]
+    recv(yin.at[1:ns], tail_sem.at[1])
     for d, f in others:
-        recv(yin.at[2 * d + f], yrecv.at[2 * d + f])
         total = total + yin[2 * d + f]
     hid = hidden[:, pl.ds(pl.multiple_of(s * cols, LANES), cols)].astype(jnp.float32)
     mine = hid[0:n_rows]
@@ -365,15 +374,16 @@
     far = [(e, d, f) for e in (2, 1, 3, 0) for d in (2, 1, 3, 0) for f in (0, 1) if (e, d, f) != (0, 0, 0)]
     far.sort(key=lambda t: -(min(t[0], ny - t[0]) + min(t[1], nx - t[1])))
     for e, d, f in far:
-        k = (e * nx + d) * 2 + f
-        send(obuf.at[me], obuf.at[me], osend.at[k], orecv.at[k], {"ctx": yy(e), "seq": xx(d) * 2 + (1 - c if f else c)})
-    for e, d, f in reversed(far):
-        recv(obuf.at[yy(-e) * ns + xx(-d) * 2 + (1 - c if f else c)], orecv.at[(e * nx + d) * 2 + f])
+        send(obuf.at[me], obuf.at[me], tail_sem.at[2], tail_sem.at[3], {"ctx": yy(e), "seq": xx(d) * 2 + (1 - c if f else c)})
+    recv(obuf.at[1:ny * ns], tail_sem.at[3])
     for s_ in range(ns):
         out[:, s_ * cols:(s_ + 1) * cols] = jnp.concatenate(
             [obuf[y_ * ns + s_].astype(jnp.float32) for y_ in range(ny)], axis=0).astype(jnp.bfloat16)
-    for copy in sends:
-        copy.wait_send()
+    sent(qbuf.at[0, 0:3, 0], gsend.at[0])
+    sent(qbuf.at[:, 0:3], gsend.at[1])
+    sent(inbox, rsend.at[0])
+    sent(ybuf.at[1:ns], tail_sem.at[0])
+    sent(obuf.at[1:ny * ns], tail_sem.at[2])
     for copy in swap:
         copy.wait_send()
 
@@ -404,13 +414,15 @@
         import functools
         out = pl.pallas_call(
             functools.partial(decode_kernel, ny, ns),
-            out_shape=jax.ShapeDtypeStruct(hidden.shape, bf),
-            in_specs=[pl.BlockSpec(memory_space=pltpu.SMEM), vmem, anyw, anyw, anyw, anyw, anyw, anyw, anyw],
+            out_shape=pltpu.VMEM(hidden.shape, bf),
+            in_specs=[anyw, anyw, anyw, anyw, anyw, anyw, anyw, anyw, anyw],
             out_specs=vmem,
             scratch_shapes=[
+                pltpu.SMEM(lengths.shape, jnp.int32),
+                pltpu.VMEM(hidden.shape, bf),
                 pltpu.VMEM((nb, 2 * t_own, wide), bf),
                 pltpu.VMEM((nb, rope_dim, 2 * t_own), bf),
-                pltpu.VMEM((2, nb // 4, 2, nx, 16, wide), bf),
+                pltpu.VMEM((2, nb // 4, 2, nx, latent // 8 + 8, LANES), bf),
                 pltpu.VMEM((2, ny, nx, unit, LANES), f32),
                 pltpu.VMEM((2, 15, unit, LANES), f32),
                 pltpu.VMEM((nh // 2,) + w_uk.shape[1:], bf),
@@ -422,8 +434,8 @@
                 pltpu.VMEM((ns, n_rows, cols), f32),
                 pltpu.VMEM((ns, n_rows, cols), f32),
                 pltpu.VMEM((ny * ns, n_rows, cols), bf),
-                dma((5,)), dma((d_model // 256,)), dma((nh // 4,)), dma((2,)), dma((2,)), dma((4, 5, 4)), dma((4, 5, 4)), dma((2, 15)), dma((2, 15)),
-                dma((ns,)), dma((ns,)), dma((ny * ns,)), dma((ny * ns,)),
+                dma((7,)), dma((d_model // 256,)), dma((nh // 4,)), dma((2,)), dma((2,)), dma((2,)), dma((4, 4)), dma((1,)), dma((2, 9)),
+                dma((4,)),
             ],
             compiler_params=pltpu.CompilerParams(collective_id=0, has_side_effects=True, vmem_limit_bytes=60 * 2 ** 20),
         )(lengths, hidden, w_uq.reshape(d_model, 2, nh // 2, -1), wqr_t, w_uk, latent_cache, rope_t, w_uv, w_out.reshape(-1, d_model))

time: 60.1 us -> 53.3 us (0.89)
  Pallas kernels: 58.4 us -> 52.5 us
  local copies, waits for them, and re-layouts: 1.59 us -> 0.67 us
    pallas_call x1, Pallas kernels: 58.4 us -> 52.5 us  [local_step(): pl.pallas_call(functools.partial(decode_kernel, ny, ns), out_shape=pltpu....]
    unnamed x1, local copies, waits for them, and re-layouts: 1.59 us -> 0.67 us
where the time goes in v4:
time: 53.3 us; the launch traced here: 53.2 us
  Pallas kernels  52.5 us (98%)
  local copies, waits for them, and re-layouts  0.67 us (1%)
    pallas_call x1, Pallas kernels, local_step(): pl.pallas_call(functools.partial(decode_kernel, ny, ns), out_shape=pltpu....  52.5 us

profile of v4, /device:TPU:97, one launch (start us, length us, event | category | flops | bytes accessed | tf_op | source)
XLA Modules:
  0.0 53.2 jit_solution(17767619956029962578)
XLA Ops:
  0.0 52.5 %shard_map.91 = bf16[16,5120]{1,0:T(8,128)(2,1)S(1)} custom-call(s32[16]{0:T(128)} %lens_in.1, bf16[16,5120]{1,0:T(8,128)(2,1)} %hidden_in.1, bf16[5120,2,8,128]{3,2,1,0:T(8,128)(2,1)} %bitcast.4, bf16[16,64,5120]{2,1,0:T(8,128)(2,1)} %bitcast.6, bf16[16,128,512]{2,1,0:T(8,128)(2,1)} %wuk.1, bf16[16,256,512]{2,1,0:T(8,128)(2,1)} %cache.1, ...), custom_call_target="tpu_custom_call" | custom-call | tf_op jit(solution)/shard_map/pallas_call | solution.py:415
  52.5 0.7 %copy.11 = bf16[16,5120]{1,0:T(8,128)(2,1)} copy(bf16[16,5120]{1,0:T(8,128)(2,1)S(1)} %shard_map.91) | data formatting | bytes 327680

commit v5 on v4

--- a/solution.py
+++ b/solution.py
@@ -9,6 +9,14 @@
 MAX_FLOOR = -1.5e38
 LANES = 128
 MESH = pl.DeviceIdType.MESH
+SUB = 8
+UNIT = 32
+PACK = 16
+OTHERS = (2, 1, 3)
+
+
+def block(i, n):
+    return slice(i * n, (i + 1) * n)
 
 
 def decode_kernel(ny, ns, lens_in, hidden_in, wuq, wqr, wuk, cache, rope, wuv, wout, out,
@@ -135,8 +143,8 @@
     q_lat = jnp.dot(big, wukb[...].reshape(half_h * nope, latent), preferred_element_type=jnp.float32).astype(jnp.bfloat16)
     for j in range(half_b // 2):
         for n in range(latent // LANES):
-            qbuf[rb, j, hb, x, 16 * n:16 * n + 16, :] = q_lat[16 * j:16 * j + 16, LANES * n:LANES * n + LANES]
-        sides = [q_rope[16 * j + 8 * i:16 * j + 8 * i + 8] for i in range(2)]
+            qbuf[rb, j, hb, x, block(n, PACK), :] = q_lat[block(j, PACK), block(n, LANES)]
+        sides = [q_rope[block(2 * j + i, SUB)] for i in range(2)]
         qbuf[rb, j, hb, x, 64:72, :] = jnp.concatenate(sides, axis=1).astype(jnp.bfloat16)
 
 
@@ -163,7 +171,7 @@
         return qbuf.at[r_, j, h_, xx(-d_x)]
 
     def hop(j, stage, ref, along_x):
-        for d in (2, 1, 3):
+        for d in OTHERS:
             send(ref, ref, gsend.at[1 if stage else 0], grecv.at[j, 0 if stage else d], at_x(d) if along_x else at_y(d))
 
     for a in range(2):
@@ -172,7 +180,7 @@
         for j in (a, a + 2):
             hop(j, 1, cell(j, 0, 0), j >= 2)
     for a in range(2):
-        for e in (1, 3, 2):
+        for e in reversed(OTHERS):
             for j in (a, a + 2):
                 recv(cell(j, e, 0), grecv.at[j, e])
                 hop(j, 1 + e, cell(j, e, 0), j >= 2)
@@ -195,25 +203,25 @@
 
     base = (y * ns + 2 * x) * t_own
     n_head = qbuf.shape[2] * qbuf.shape[3] * 8
-    lane = lax.broadcasted_iota(jnp.int32, (8, LANES), 1)
+    lane = lax.broadcasted_iota(jnp.int32, (SUB, LANES), 1)
     n_slab = latent // LANES
 
     def stats(groups):
-        tile = jnp.zeros((8, LANES), jnp.float32)
+        tile = jnp.zeros((SUB, LANES), jnp.float32)
         for i, (m_, l_) in enumerate(groups):
             tile = jnp.where((lane >= 32 * i) & (lane < 32 * i + 16), m_, tile)
             tile = jnp.where((lane >= 32 * i + 16) & (lane < 32 * i + 32), l_, tile)
         return tile
 
     def attend(*pairs):
-        first = lax.broadcasted_iota(jnp.int32, (n_pos, 2 * n_head), 1) % 16 < 8
-        first_row = lax.broadcasted_iota(jnp.int32, (1, 2 * n_head), 1) % 16 < 8
+        first = lax.broadcasted_iota(jnp.int32, (n_pos, 2 * n_head), 1) % PACK < SUB
+        first_row = lax.broadcasted_iota(jnp.int32, (1, 2 * n_head), 1) % PACK < SUB
         pos = lax.broadcasted_iota(jnp.int32, (n_pos, 2 * n_head), 0)
         b0s = [4 * r + 2 * (1 - cls) for cls, r in pairs]
         scores = []
         for (cls, r), b0 in zip(pairs, b0s):
             r_, j_ = r // 2, 1 - cls + 2 * (r % 2)
-            slabs = [qbuf[r_, j_, :, :, 16 * n:16 * n + 16, :].reshape(2 * n_head, LANES) for n in range(n_slab)]
+            slabs = [qbuf[r_, j_, :, :, block(n, PACK), :].reshape(2 * n_head, LANES) for n in range(n_slab)]
             side = qbuf[r_, j_, :, :, 64:72, :]
             side = jnp.concatenate([side, side], axis=2).reshape(2 * n_head, LANES)
             q2 = jnp.concatenate(slabs + [side], axis=1)
@@ -236,10 +244,10 @@
                 ml = []
                 for g in range(4):
                     k = ((g % 2) * nx + x_) * 16 + 8 * (g // 2)
-                    ml.append((ml_cols[k:k + 8, 0:1], ml_cols[k:k + 8, 1:2]))
+                    ml.append((ml_cols[k:k + SUB, 0:1], ml_cols[k:k + SUB, 1:2]))
                     for n in range(n_slab):
-                        part[cls, r, x_, 32 * n + 8 * g:32 * n + 8 * g + 8, :] = acc[g // 2][k:k + 8, LANES * n:LANES * n + LANES]
-                part[cls, r, x_, 32 * n_slab:32 * n_slab + 8, :] = stats(ml)
+                        part[cls, r, x_, block(4 * n + g, SUB), :] = acc[g // 2][k:k + SUB, block(n, LANES)]
+                part[cls, r, x_, block(4 * n_slab, SUB), :] = stats(ml)
 
     def merge(items):
         new = []
@@ -249,8 +257,8 @@
             tiles = [ref[row:row + 8, :] for ref in refs]
             ml = []
             for g in range(4):
-                ms = [jnp.broadcast_to(t[:, 32 * g:32 * g + 1], (8, LANES)) for t in tiles]
-                ls = [jnp.broadcast_to(t[:, 32 * g + 16:32 * g + 17], (8, LANES)) for t in tiles]
+                ms = [jnp.broadcast_to(t[:, UNIT * g:UNIT * g + 1], (SUB, LANES)) for t in tiles]
+                ls = [jnp.broadcast_to(t[:, UNIT * g + PACK:UNIT * g + PACK + 1], (SUB, LANES)) for t in tiles]
                 m = ms[0]
                 for other_m in ms[1:]:
                     m = jnp.maximum(m, other_m)
@@ -280,24 +288,30 @@
     def yy(d):
         return (y + d + ny) % ny
 
+    def a_sign(r):
+        return 1 - 2 * (r % 2)
+
+    def a_slot(r, sg):
+        return 4 + 2 * r + (1 - sg) // 2
+
     def a_first(r):
-        sg = 1 - 2 * (r % 2)
+        sg = a_sign(r)
         rs_send(0, r, xx(2), r, r, at_x(sg))
-        rs_send(0, r, xx(-sg), 4 + 2 * r + (1 + sg) // 2, 4 + r, at_x(-sg))
+        rs_send(0, r, xx(-sg), a_slot(r, -sg), 4 + r, at_x(-sg))
 
     def a_second(r):
-        sg = 1 - 2 * (r % 2)
+        sg = a_sign(r)
         rs_merge((0, r, xx(sg), r, 1, r))
-        rs_send(0, r, xx(sg), 4 + 2 * r + (1 - sg) // 2, 4 + r, at_x(sg))
+        rs_send(0, r, xx(sg), a_slot(r, sg), 4 + r, at_x(sg))
 
     def b_send(d, odd):
         for x_ in range(odd, nx, 2):
-            rs_send(1, yy(d), x_, 4 + 2 * x_ + (1 - d) // 2, 4 + x_, at_y(d))
+            rs_send(1, yy(d), x_, a_slot(x_, d), 4 + x_, at_y(d))
 
     def b_second(d, odd):
         rs_merge(*[(1, yy(d), x_, x_, 1, x_) for x_ in range(odd, nx, 2)])
         for x_ in range(odd, nx, 2):
-            rs_send(1, yy(d), x_, 4 + 2 * x_ + (1 - d) // 2, 4 + x_, at_y(d))
+            rs_send(1, yy(d), x_, a_slot(x_, d), 4 + x_, at_y(d))
 
     def pair(cls, r, x_, k):
         return (cls, r, x_, 4 + 2 * k, 2, 4 + k)
@@ -322,7 +336,7 @@
     a_second(yy(1))
     a_second(yy(-1))
     a_second(y)
-    for d in (2, 1, 3):
+    for d in OTHERS:
         rs_merge(pair(0, yy(d), x, yy(d)), pair(1, y, xx(d), xx(d)))
         rs_send(0, yy(d), x, 11 + d, 8, at_y(d))
         rs_send(1, y, xx(d), 11 + d, 8, at_x(d))
@@ -332,10 +346,10 @@
     rows = []
     for cls in (1, 0):
         own = part.at[cls, y, x]
-        st = own[32 * n_slab:32 * n_slab + 8, :]
+        st = own[block(4 * n_slab, SUB), :]
         for g in range(4):
-            inv = jnp.broadcast_to(st[:, 32 * g + 16:32 * g + 17], (8, LANES))
-            rows.append(jnp.concatenate([own[32 * n + 8 * g:32 * n + 8 * g + 8, :] / inv for n in range(n_slab)], axis=1))
+            inv = jnp.broadcast_to(st[:, UNIT * g + PACK:UNIT * g + PACK + 1], (SUB, LANES))
+            rows.append(jnp.concatenate([own[block(4 * n + g, SUB), :] / inv for n in range(n_slab)], axis=1))
     o_l = jnp.concatenate(rows, axis=0).astype(jnp.bfloat16)
     n_own = o_l.shape[0]
     local[3].wait()
@@ -348,10 +362,10 @@
     pj = lax.broadcasted_iota(jnp.int32, (16 * nh, n_own), 1)
     perm = jnp.where((pj % nh == pi // 16) & (pj // nh == pi % 16), 1.0, 0.0).astype(jnp.bfloat16)
     vp = jnp.dot(perm, v, preferred_element_type=jnp.float32).astype(jnp.bfloat16)
-    lhs = jnp.concatenate([vp[16 * h:16 * h + 16] for h in range(nh)], axis=1)
+    lhs = jnp.concatenate([vp[block(h, PACK)] for h in range(nh)], axis=1)
     local[4].wait()
     n_rows = n_own // nh
-    others = [(d, f) for d in (2, 1, 3, 0) for f in (0, 1) if (d, f) != (0, 0)]
+    others = [(d, f) for d in OTHERS + (0,) for f in range(2) if d or f]
     for d, f in others + [(0, 0)]:
         s_ = xx(d) * 2 + (1 - c if f else c)
         piece = jnp.dot(lhs, woutb[:, pl.ds(pl.multiple_of(s_ * cols, LANES), cols)], preferred_element_type=jnp.float32)
@@ -371,7 +385,7 @@
         mine = jnp.where(y == y_, hid[n_rows * y_:n_rows * y_ + n_rows], mine)
     obuf[y * ns + s] = (mine + total).astype(jnp.bfloat16)
     me = y * ns + s
-    far = [(e, d, f) for e in (2, 1, 3, 0) for d in (2, 1, 3, 0) for f in (0, 1) if (e, d, f) != (0, 0, 0)]
+    far = [(e, d, f) for e in OTHERS + (0,) for d in OTHERS + (0,) for f in range(2) if e or d or f]
     far.sort(key=lambda t: -(min(t[0], ny - t[0]) + min(t[1], nx - t[1])))
     for e, d, f in far:
         send(obuf.at[me], obuf.at[me], tail_sem.at[2], tail_sem.at[3], {"ctx": yy(e), "seq": xx(d) * 2 + (1 - c if f else c)})

time: 53.3 us -> 54 us (1.013)
  Pallas kernels: 52.5 us -> 53.2 us
    pallas_call x1, Pallas kernels: 52.5 us -> 53.2 us  [local_step(): pl.pallas_call(functools.partial(decode_kernel, ny, ns), out_shape=pltpu....]
where the time goes in v5:
time: 54 us; the launch traced here: 53.9 us
  Pallas kernels  53.2 us (99%)
  local copies, waits for them, and re-layouts  0.67 us (1%)
    pallas_call x1, Pallas kernels, local_step(): pl.pallas_call(functools.partial(decode_kernel, ny, ns), out_shape=pltpu....  53.2 us

profile of v5, /device:TPU:97, one launch (start us, length us, event | category | flops | bytes accessed | tf_op | source)
XLA Modules:
  0.0 53.9 jit_solution(16922782660113840085)
XLA Ops:
  0.0 53.2 %shard_map.91 = bf16[16,5120]{1,0:T(8,128)(2,1)S(1)} custom-call(s32[16]{0:T(128)} %lens_in.1, bf16[16,5120]{1,0:T(8,128)(2,1)} %hidden_in.1, bf16[5120,2,8,128]{3,2,1,0:T(8,128)(2,1)} %bitcast.4, bf16[16,64,5120]{2,1,0:T(8,128)(2,1)} %bitcast.6, bf16[16,128,512]{2,1,0:T(8,128)(2,1)} %wuk.1, bf16[16,256,512]{2,1,0:T(8,128)(2,1)} %cache.1, ...), custom_call_target="tpu_custom_call" | custom-call | tf_op jit(solution)/shard_map/pallas_call | solution.py:429
  53.2 0.7 %copy.11 = bf16[16,5120]{1,0:T(8,128)(2,1)} copy(bf16[16,5120]{1,0:T(8,128)(2,1)S(1)} %shard_map.91) | data formatting | bytes 327680

commit v6 on v5

--- a/solution.py
+++ b/solution.py
@@ -180,7 +180,7 @@
         for j in (a, a + 2):
             hop(j, 1, cell(j, 0, 0), j >= 2)
     for a in range(2):
-        for e in reversed(OTHERS):
+        for e in (1, 3, 2):
             for j in (a, a + 2):
                 recv(cell(j, e, 0), grecv.at[j, e])
                 hop(j, 1 + e, cell(j, e, 0), j >= 2)

time: 54 us -> 53.3 us (0.987)
  Pallas kernels: 53.2 us -> 52.5 us
    pallas_call x1, Pallas kernels: 53.2 us -> 52.5 us  [local_step(): pl.pallas_call(functools.partial(decode_kernel, ny, ns), out_shape=pltpu....]
where the time goes in v6:
time: 53.3 us; the launch traced here: 53.2 us
  Pallas kernels  52.5 us (98%)
  local copies, waits for them, and re-layouts  0.67 us (1%)
    pallas_call x1, Pallas kernels, local_step(): pl.pallas_call(functools.partial(decode_kernel, ny, ns), out_shape=pltpu....  52.5 us

profile of v6, /device:TPU:97, one launch (start us, length us, event | category | flops | bytes accessed | tf_op | source)
XLA Modules:
  0.0 53.2 jit_solution(17767619956029962578)
XLA Ops:
  0.0 52.5 %shard_map.91 = bf16[16,5120]{1,0:T(8,128)(2,1)S(1)} custom-call(s32[16]{0:T(128)} %lens_in.1, bf16[16,5120]{1,0:T(8,128)(2,1)} %hidden_in.1, bf16[5120,2,8,128]{3,2,1,0:T(8,128)(2,1)} %bitcast.4, bf16[16,64,5120]{2,1,0:T(8,128)(2,1)} %bitcast.6, bf16[16,128,512]{2,1,0:T(8,128)(2,1)} %wuk.1, bf16[16,256,512]{2,1,0:T(8,128)(2,1)} %cache.1, ...), custom_call_target="tpu_custom_call" | custom-call | tf_op jit(solution)/shard_map/pallas_call | solution.py:429
  52.5 0.7 %copy.11 = bf16[16,5120]{1,0:T(8,128)(2,1)} copy(bf16[16,5120]{1,0:T(8,128)(2,1)S(1)} %shard_map.91) | data formatting | bytes 327680
